TPU v7x, 256 devices: a whole 4x4x8 slice. The times are simulated.
256 devices in a mesh: blk: 32 (over x, z), pair: 8 (over y, core).
Axes of the slice: x: 4, y: 4, z: 8, core: 2. Of those that a mesh axis runs over, the one named last changes fastest.
Arguments:
- features: float32 [64, 262144], P(None, 'blk'), may hold values from -6 to 6
- inv_scale: float32 [64], replicated, may hold values from 0.03125 to 20
- signal: float32 [1], replicated, may hold values from 0.110485435 to 0.44194174
- noise_var: float32 [262144], P('blk'), may hold values from 0.5 to 2
- right_side: float32 [32, 262144], P(None, 'blk'), may hold values from -30 to 30
- block_pairs: int32 [512, 2], P(('blk', 'pair')), may hold values from -1 to 127, as said below
Outputs:
- solution: float32 [32, 262144], P(None, 'blk')
- residual: float32 [32, 262144], P(None, 'blk')
Inputs may be any that keep to these rules, and one draw needn't show every extreme that they name: `block_pairs`: rows run over the blk index, then the pair index, then 2 slots of one device. In each device's slots the live pairs come first; dead slots hold -1 in both columns. A live pair (i, j) has block i among blocks blk index * 4 to blk index * 4 + 3 of the device's blk index, and j equal to i or i + 1. Every block's pair (i, i) is listed once and no pair twice. In each blk index some device has all its slots live.
All inputs are finite; a program needn't handle non-finite values.
Results may differ from a plain program's by a relative error of at most 0.0011.
Values sent between devices are 32-bit elements; how exact they have to be, the bound alone decides.
A program may use at most 64 MiB of HBM per device.

v0:
```python
import jax
import jax.numpy as jnp
from jax import lax
from jax.sharding import PartitionSpec as P

BS = 2048
ITERS = 2


root_three = 1.7320508075688772
taper_radius = 2.0


def passed_along(block, axis, distance):
    devices = range(lax.axis_size(axis))
    route = [(i - distance, i) for i in devices if i - distance in devices]
    return lax.ppermute(block, axis, route)


def copy_for_each(array, axis):
    count = lax.axis_size(axis)
    return lax.all_to_all(
        jnp.broadcast_to(array[None], (count, *array.shape)), axis, 0, 0, tiled=True
    )


def joined_along(parts, dim):
    shape = list(parts.shape[1:])
    shape[dim] *= parts.shape[0]
    return jnp.moveaxis(parts, 0, dim).reshape(shape)


def gathered_copies(array, axis, dim):
    parts = copy_for_each(array, axis)
    return joined_along(parts, dim)


def in_blocks(array, dim, count):
    before, after = (array.shape[:dim], array.shape[dim + 1 :])
    return jnp.moveaxis(array.reshape(*before, count, -1, *after), dim, 0)


def summed_on_arrival(array, axis, dim):
    parts = in_blocks(array, dim, lax.axis_size(axis))
    arrived = lax.all_to_all(parts, axis, split_axis=0, concat_axis=0, tiled=True)
    return arrived.sum(axis=0)


def one_gather(arrays, axis, dims):
    vector = jnp.concatenate([a.reshape(-1) for a in arrays])
    lines, at, gathered = (lax.all_gather(vector, axis), 0, [])
    for a, dim in zip(arrays, dims):
        parts = lines[:, at : at + a.size].reshape(-1, *a.shape)
        gathered.append(joined_along(parts, dim))
        at += a.size
    return tuple(gathered)


def of_everyone(array, axis):
    everything = copy_for_each(array, axis)
    return jnp.sum(everything, axis=0)


def in_one(arrays, axis):
    vector, at, gathered = (jnp.concatenate([a.reshape(-1) for a in arrays]), 0, [])
    running = of_everyone(vector, axis)
    for a in arrays:
        gathered.append(running[at : at + a.size].reshape(a.shape))
        at += a.size
    return tuple(gathered)


def kernel_tile(left_scaled, right_scaled, amplitude):
    cross = lax.dot_general(
        left_scaled,
        right_scaled,
        (((0,), (0,)), ((), ())),
        precision=lax.Precision.HIGHEST,
        preferred_element_type=jnp.float32,
    )
    left_norms = jnp.sum(left_scaled * left_scaled, axis=0)
    right_norms = jnp.sum(right_scaled * right_scaled, axis=0)
    squared = (left_norms[:, None] + right_norms[None, :] - 2.0 * cross) / left_scaled.shape[0]
    distance = jnp.sqrt(jnp.maximum(squared, 0.0))
    stretched = root_three * distance
    ratio = distance / taper_radius
    taper = jnp.maximum(1.0 - ratio, 0.0) ** 4 * (1.0 + 4.0 * ratio)
    return amplitude * (1.0 + stretched) * jnp.exp(-stretched) * taper


def block_terms(left_scaled, right_scaled, left_dir, right_dir, amplitude):
    block_rows = left_scaled.shape[1]
    row_step = min(512, block_rows)
    left_half = left_dir.astype(jnp.bfloat16)
    right_half = right_dir.astype(jnp.bfloat16)

    def rows_visit(position, carried):
        toward_left, toward_right, row_sums, col_sums = carried
        offset = position * row_step
        kernel_rows = kernel_tile(
            lax.dynamic_slice_in_dim(left_scaled, offset, row_step, 1), right_scaled, amplitude
        )
        rows_half = kernel_rows.astype(jnp.bfloat16)
        product = lax.dot_general(
            right_half, rows_half, (((1,), (1,)), ((), ())), preferred_element_type=jnp.float32
        )
        toward_left = lax.dynamic_update_slice_in_dim(toward_left, product, offset, 1)
        toward_right = toward_right + jnp.dot(
            lax.dynamic_slice_in_dim(left_half, offset, row_step, 1),
            rows_half,
            preferred_element_type=jnp.float32,
        )
        row_sums = lax.dynamic_update_slice_in_dim(
            row_sums, jnp.sum(kernel_rows, axis=1), offset, 0
        )
        col_sums = col_sums + jnp.sum(kernel_rows, axis=0)
        return (toward_left, toward_right, row_sums, col_sums)

    zeros_dir = jnp.zeros(left_dir.shape, jnp.float32)
    zeros_row = jnp.zeros((block_rows,), jnp.float32)
    return lax.fori_loop(
        0, block_rows // row_step, rows_visit, (zeros_dir, zeros_dir, zeros_row, zeros_row)
    )


def body(features, inv_scale, signal, noise_var, right_side, block_pairs):
    local_rows = features.shape[1]
    blocks_here = local_rows // BS
    amplitude = signal[0]
    scaled = features * inv_scale[:, None]
    beyond = passed_along(scaled[:, :BS], "blk", -1)
    reach_scaled = jnp.concatenate([scaled, beyond], axis=1)
    base_block = lax.axis_index("blk") * blocks_here
    members = lax.axis_size("pair")
    listing = gathered_copies(block_pairs, "pair", 0)
    living = (listing[:, 0] >= 0).astype(jnp.int32)
    ranked = jnp.cumsum(living) - living
    wanted = lax.axis_index("pair") + members * jnp.arange(block_pairs.shape[0], dtype=jnp.int32)
    matched = (ranked[None, :] == wanted[:, None]) & (living[None, :] > 0)
    chosen = jnp.sum(jnp.where(matched[:, :, None], listing[None, :, :], 0), axis=1)
    my_pairs = jnp.where(jnp.any(matched, axis=1)[:, None], chosen, -1)
    active = jnp.maximum((jnp.sum(living) - lax.axis_index("pair") + members - 1) // members, 0)
    row_local = my_pairs[:, 0] - base_block
    col_local = my_pairs[:, 1] - base_block
    solution = jnp.zeros_like(right_side)
    residual = right_side
    direction = right_side
    norm_now = of_everyone(jnp.sum(residual * residual, axis=1), "blk")
    for iteration in range(ITERS):
        ahead_dir = passed_along(direction[:, :BS], "blk", -1)
        reach_dir = jnp.concatenate([direction, ahead_dir], axis=1)

        def visit(slot_index, summed):
            row_start = row_local[slot_index] * BS
            col_start = col_local[slot_index] * BS
            crossing = (row_local[slot_index] != col_local[slot_index]).astype(jnp.float32)
            left_dir = lax.dynamic_slice_in_dim(reach_dir, row_start, BS, 1)
            right_dir = lax.dynamic_slice_in_dim(reach_dir, col_start, BS, 1)
            toward_left, toward_right, row_sums, col_sums = block_terms(
                lax.dynamic_slice_in_dim(reach_scaled, row_start, BS, 1),
                lax.dynamic_slice_in_dim(reach_scaled, col_start, BS, 1),
                left_dir,
                right_dir,
                amplitude,
            )
            term_left = toward_left + crossing * row_sums[None, :] * left_dir
            term_right = crossing * (toward_right + col_sums[None, :] * right_dir)
            summed = lax.dynamic_update_slice_in_dim(
                summed, lax.dynamic_slice_in_dim(summed, row_start, BS, 1) + term_left, row_start, 1
            )
            summed = lax.dynamic_update_slice_in_dim(
                summed,
                lax.dynamic_slice_in_dim(summed, col_start, BS, 1) + term_right,
                col_start,
                1,
            )
            return summed

        summed = lax.fori_loop(0, active, visit, jnp.zeros(reach_dir.shape, jnp.float32))
        own_part = summed[:, :local_rows]
        next_part = summed[:, local_rows:]
        own_share = summed_on_arrival(own_part, "pair", 1)
        next_share = summed_on_arrival(next_part, "pair", 1)
        arrived = passed_along(next_share, "blk", 1)
        own_sum, entering = one_gather((own_share, arrived), "pair", (1, 1))
        coupled = jnp.concatenate([own_sum[:, :BS] + entering, own_sum[:, BS:]], axis=1)
        applied = noise_var[None, :] * direction + coupled
        last_turn = iteration + 1 == ITERS
        curvature, mixed_sum, image_sum = in_one(
            (
                jnp.sum(direction * applied, axis=1),
                jnp.sum(residual * applied, axis=1),
                jnp.sum(applied * applied, axis=1),
            ),
            "blk",
        )
        step_size = norm_now / curvature
        solution = solution + step_size[:, None] * direction
        residual = residual - step_size[:, None] * applied
        if not last_turn:
            norm_next = norm_now - 2.0 * step_size * mixed_sum + step_size * step_size * image_sum
            direction = residual + (norm_next / norm_now)[:, None] * direction
            norm_now = norm_next
    return (solution, residual)


def solution(mesh):
    placed = (P(None, "blk"), P(), P(), P("blk"), P(None, "blk"), P(("blk", "pair"), None))
    return jax.shard_map(
        body,
        mesh=mesh,
        in_specs=placed,
        out_specs=(P(None, "blk"), P(None, "blk")),
        check_vma=False,
    )
```

profile of v0, /device:TPU:1, one launch (start us, length us, event | category | flops | bytes accessed | tf_op | source)
XLA Modules:
  0.0 351.5 jit_solution(1274253293373501559)
XLA Ops:
  8.5 6.4 %all-to-all-start.1 = ((s32[8,2,2]{1,2,0:T(2,128)}), s32[8,2,2]{1,2,0:T(2,128)S(1)}, u32[]{:S(2)}, u32[]{:S(2)}) async-start(s32[8,2,2]{1,2,0:T(2,128)} %broadcast_in_dim.53), calls=%async_computation.1 | async-start | bytes 16384 | tf_op jit(solution)/shard_map/all_to_all | solution.py:22
  15.0 1.7 slice.70
  16.6 1.4 collective-permute-start.1
  18.1 1.8 broadcast_multiply_fusion.2
  19.9 0.8 slice.88
  20.7 1.3 collective-permute-start
  24.2 2.4 collective-permute-done.1
  26.6 1.2 pad_maximum_fusion.1
  27.8 10.2 %collective-permute-done = f32[64,2048]{1,0:T(8,128)} collective-permute-done((f32[64,2048]{1,0:T(8,128)}, f32[64,2048]{1,0:T(8,128)}, u32[]{:S(2)}, u32[]{:S(2)}) %collective-permute-start) | collective-permute-done | bytes 524320 | tf_op jit(solution)/shard_map/ppermute | solution.py:17
  38.0 2.7 pad_maximum_fusion
  40.7 1.2 broadcast.254.clone
  41.9 55.2 %while.101 = (s32[]{:T(128)}, f32[32,10240]{1,0:T(8,128)}, s32[]{:T(128)}, s32[2]{0:T(128)S(1)}, f32[64,10240]{1,0:T(8,128)}, /*index=5*/s32[2]{0:T(128)S(1)}, f...) while((s32[]{:T(128)}, f32[32,10240]{1,0:T(8,128)}, ...), condition=%wide.region_13.14_spmd, body=%wide.region_6.13_spmd.sunk | while | flops 963511296 | bytes 12913883 | solution.py:179
  45.8 1.1 dynamic-slice_convert_fusion.6
  47.0 2.1 multiply_reduce_fusion.14
  49.1 44.5 %while.104 = (s32[]{:T(128)}, f32[32,2048]{1,0:T(8,128)S(1)}, f32[32,2048]{1,0:T(8,128)S(1)}, f32[2048]{0:T(1024)S(1)}, f32[2048]{0:T(1024)S(1)}, /*index=5*/f32...) while((s32[]{:T(128)}, f32[32,2048]{1,0:T(8,128)S(1)}, ...), condition=%wide.region_12.12_spmd.clone, body=%wide.region_8.11_spmd.clone.sunk | while | flops 962790400 | bytes 7882982 | solution.py:121
  49.1 9.6 %fusion.54 = (f32[2048]{0:T(1024)S(1)}, f32[512]{0:T(512)S(1)}, bf16[512,2048]{1,0:T(8,128)(2,1)S(1)}) fusion(f32[64,2048]{1,0:T(8,128)} %get-tuple-element.1381, f32[64,2048]{1,0:T(8,128)S(1)} %get-tuple-element.1379, s32[]{:T(128)S(6)} %select_n.115, f32[2048]{0:T(1024)S(1)} %get-tuple-element.1380, f32[512]{0:T(512)S(1)} %multiply_reduce_fusion.17, ...), kind=kOutput, calls=%fused_computation.77.clone.1 | convolution fusion | flops 828372480 | bytes 2773000 | tf_op jit(solution)/shard_map/while/body/while/body/eval_jaxpr/dot_general | solution.py:74
  60.3 9.6 %fusion.54 = (f32[2048]{0:T(1024)S(1)}, f32[512]{0:T(512)S(1)}, bf16[512,2048]{1,0:T(8,128)(2,1)S(1)}) fusion(f32[64,2048]{1,0:T(8,128)} %get-tuple-element.1381, f32[64,2048]{1,0:T(8,128)S(1)} %get-tuple-element.1379, s32[]{:T(128)S(6)} %select_n.115, f32[2048]{0:T(1024)S(1)} %get-tuple-element.1380, f32[512]{0:T(512)S(1)} %multiply_reduce_fusion.17, ...), kind=kOutput, calls=%fused_computation.77.clone.1 | convolution fusion | flops 828372480 | bytes 2773000 | tf_op jit(solution)/shard_map/while/body/while/body/eval_jaxpr/dot_general | solution.py:74
  71.4 9.6 %fusion.54 = (f32[2048]{0:T(1024)S(1)}, f32[512]{0:T(512)S(1)}, bf16[512,2048]{1,0:T(8,128)(2,1)S(1)}) fusion(f32[64,2048]{1,0:T(8,128)} %get-tuple-element.1381, f32[64,2048]{1,0:T(8,128)S(1)} %get-tuple-element.1379, s32[]{:T(128)S(6)} %select_n.115, f32[2048]{0:T(1024)S(1)} %get-tuple-element.1380, f32[512]{0:T(512)S(1)} %multiply_reduce_fusion.17, ...), kind=kOutput, calls=%fused_computation.77.clone.1 | convolution fusion | flops 828372480 | bytes 2773000 | tf_op jit(solution)/shard_map/while/body/while/body/eval_jaxpr/dot_general | solution.py:74
  82.5 9.6 %fusion.54 = (f32[2048]{0:T(1024)S(1)}, f32[512]{0:T(512)S(1)}, bf16[512,2048]{1,0:T(8,128)(2,1)S(1)}) fusion(f32[64,2048]{1,0:T(8,128)} %get-tuple-element.1381, f32[64,2048]{1,0:T(8,128)S(1)} %get-tuple-element.1379, s32[]{:T(128)S(6)} %select_n.115, f32[2048]{0:T(1024)S(1)} %get-tuple-element.1380, f32[512]{0:T(512)S(1)} %multiply_reduce_fusion.17, ...), kind=kOutput, calls=%fused_computation.77.clone.1 | convolution fusion | flops 828372480 | bytes 2773000 | tf_op jit(solution)/shard_map/while/body/while/body/eval_jaxpr/dot_general | solution.py:74
  93.5 1.8 add_dynamic-update-slice_fusion.8
  95.3 1.8 add_dynamic-update-slice_fusion.9
  97.1 1.1 slice.72
  98.3 0.8 copy.45
  99.0 5.4 %all-to-all-start.3 = ((f32[8,32,256]{2,1,0:T(8,128)}), f32[8,32,256]{2,1,0:T(8,128)S(1)}, u32[]{:S(2)}, u32[]{:S(2)}) async-start(f32[8,32,256]{2,1,0:T(8,128)} %copy.45), calls=%async_computation.3 | async-start | bytes 524288 | tf_op jit(solution)/shard_map/all_to_all | solution.py:45
  105.2 1.6 copy.44
  106.7 4.2 %all-to-all-done.3 = f32[8,32,256]{2,1,0:T(8,128)S(1)} async-done(((f32[8,32,256]{2,1,0:T(8,128)}), f32[8,32,256]{2,1,0:T(8,128)S(1)}, u32[]{:S(2)}, u32[]{:S(2)}) %all-to-all-start.3) | async-done | bytes 262176 | tf_op jit(solution)/shard_map/all_to_all | solution.py:45
  110.9 4.5 %all-to-all-start.2 = ((f32[8,32,1024]{2,1,0:T(8,128)}), f32[8,32,1024]{2,1,0:T(8,128)S(1)}, u32[]{:S(2)}, u32[]{:S(2)}) async-start(f32[8,32,1024]{2,1,0:T(8,128)} %copy.44), calls=%async_computation.2 | async-start | bytes 2097152 | tf_op jit(solution)/shard_map/all_to_all | solution.py:45
  115.5 3.2 collective-permute-start.2
  118.7 1.0 collective-permute-done.2
  119.7 10.7 %all-to-all-done.2 = f32[8,32,1024]{2,1,0:T(8,128)S(1)} async-done(((f32[8,32,1024]{2,1,0:T(8,128)}), f32[8,32,1024]{2,1,0:T(8,128)S(1)}, u32[]{:S(2)}, u32[]{:S(2)}) %all-to-all-start.2) | async-done | bytes 1048608 | tf_op jit(solution)/shard_map/all_to_all | solution.py:45
  131.2 28.4 %all-gather.5.cloned.1.call-done = f32[327680]{0:T(1024)} async-done(((f32[40960]{0:T(1024)}), f32[327680]{0:T(1024)}) %all-gather.5.cloned.1.call-update) | async-done | bytes 1310736 | tf_op jit(solution)/shard_map/all_gather | solution.py:51
  159.7 1.6 reshape.212
  163.6 9.5 %all-to-all-start = ((f32[32,1,32]{2,1,0:T(1,128)}), f32[32,1,32]{2,1,0:T(1,128)S(1)}, u32[]{:S(2)}, u32[]{:S(2)}) async-start(f32[32,1,32]{2,1,0:T(1,128)} %broadcast_in_dim.52), calls=%async_computation | async-start | bytes 32768 | tf_op jit(solution)/shard_map/all_to_all | solution.py:22
  173.2 8.5 %all-to-all-done = f32[32,1,32]{2,1,0:T(1,128)S(1)} async-done(((f32[32,1,32]{2,1,0:T(1,128)}), f32[32,1,32]{2,1,0:T(1,128)S(1)}, u32[]{:S(2)}, u32[]{:S(2)}) %all-to-all-start) | async-done | bytes 4128 | tf_op jit(solution)/shard_map/all_to_all | solution.py:22
  182.4 3.8 %all-to-all-start.4 = ((f32[32,1,96]{2,1,0:T(1,128)}), f32[32,1,96]{2,1,0:T(1,128)S(1)}, u32[]{:S(2)}, u32[]{:S(2)}) async-start(f32[32,1,96]{2,1,0:T(1,128)} %broadcast_in_dim.63), calls=%async_computation.4 | async-start | bytes 32768 | tf_op jit(solution)/shard_map/all_to_all | solution.py:22
  186.2 8.6 %all-to-all-done.4 = f32[32,1,96]{2,1,0:T(1,128)S(1)} async-done(((f32[32,1,96]{2,1,0:T(1,128)}), f32[32,1,96]{2,1,0:T(1,128)S(1)}, u32[]{:S(2)}, u32[]{:S(2)}) %all-to-all-start.4) | async-done | bytes 12320 | tf_op jit(solution)/shard_map/all_to_all | solution.py:22
  196.0 1.5 collective-permute-start.3
  197.5 5.6 %collective-permute-done.3 = f32[32,2048]{1,0:T(8,128)S(1)} collective-permute-done((f32[32,2048]{1,0:T(8,128)S(1)}, f32[32,2048]{1,0:T(8,128)S(1)}, u32[]{:S(2)}, u32[]{:S(2)}) %collective-permute-start.3) | collective-permute-done | bytes 262176 | tf_op jit(solution)/shard_map/ppermute | solution.py:17
  203.1 1.2 pad_maximum_fusion.2
  204.3 1.2 broadcast.254
  205.4 55.1 %while.103 = (s32[]{:T(128)}, f32[32,10240]{1,0:T(8,128)}, s32[]{:T(128)}, s32[2]{0:T(128)S(1)}, f32[64,10240]{1,0:T(8,128)}, /*index=5*/s32[2]{0:T(128)S(1)}, f...) while((s32[]{:T(128)}, f32[32,10240]{1,0:T(8,128)}, ...), condition=%wide.region_26.27_spmd, body=%wide.region_19.0_spmd.sunk | while | flops 963511296 | bytes 12913883 | solution.py:179
  209.3 1.1 dynamic-slice_convert_fusion.7
  210.4 2.1 multiply_reduce_fusion.15
  212.5 44.5 %while.105 = (s32[]{:T(128)}, f32[32,2048]{1,0:T(8,128)S(1)}, f32[32,2048]{1,0:T(8,128)S(1)}, f32[2048]{0:T(1024)S(1)}, f32[2048]{0:T(1024)S(1)}, /*index=5*/f32...) while((s32[]{:T(128)}, f32[32,2048]{1,0:T(8,128)S(1)}, ...), condition=%wide.region_25.25_spmd.clone, body=%wide.region_21.24_spmd.clone.sunk | while | flops 962790400 | bytes 7882982 | solution.py:121
  212.6 9.6 %fusion.47 = (f32[2048]{0:T(1024)S(1)}, f32[512]{0:T(512)S(1)}, bf16[512,2048]{1,0:T(8,128)(2,1)S(1)}) fusion(f32[64,2048]{1,0:T(8,128)} %get-tuple-element.1336, f32[64,2048]{1,0:T(8,128)S(1)} %get-tuple-element.1334, s32[]{:T(128)S(6)} %select_n.114, f32[2048]{0:T(1024)S(1)} %get-tuple-element.1335, f32[512]{0:T(512)S(1)} %multiply_reduce_fusion.16, ...), kind=kOutput, calls=%fused_computation.78.clone.1 | convolution fusion | flops 828372480 | bytes 2773000 | tf_op jit(solution)/shard_map/while/body/while/body/eval_jaxpr/dot_general | solution.py:74
  223.7 9.6 %fusion.47 = (f32[2048]{0:T(1024)S(1)}, f32[512]{0:T(512)S(1)}, bf16[512,2048]{1,0:T(8,128)(2,1)S(1)}) fusion(f32[64,2048]{1,0:T(8,128)} %get-tuple-element.1336, f32[64,2048]{1,0:T(8,128)S(1)} %get-tuple-element.1334, s32[]{:T(128)S(6)} %select_n.114, f32[2048]{0:T(1024)S(1)} %get-tuple-element.1335, f32[512]{0:T(512)S(1)} %multiply_reduce_fusion.16, ...), kind=kOutput, calls=%fused_computation.78.clone.1 | convolution fusion | flops 828372480 | bytes 2773000 | tf_op jit(solution)/shard_map/while/body/while/body/eval_jaxpr/dot_general | solution.py:74
  234.8 9.6 %fusion.47 = (f32[2048]{0:T(1024)S(1)}, f32[512]{0:T(512)S(1)}, bf16[512,2048]{1,0:T(8,128)(2,1)S(1)}) fusion(f32[64,2048]{1,0:T(8,128)} %get-tuple-element.1336, f32[64,2048]{1,0:T(8,128)S(1)} %get-tuple-element.1334, s32[]{:T(128)S(6)} %select_n.114, f32[2048]{0:T(1024)S(1)} %get-tuple-element.1335, f32[512]{0:T(512)S(1)} %multiply_reduce_fusion.16, ...), kind=kOutput, calls=%fused_computation.78.clone.1 | convolution fusion | flops 828372480 | bytes 2773000 | tf_op jit(solution)/shard_map/while/body/while/body/eval_jaxpr/dot_general | solution.py:74
  245.9 9.6 %fusion.47 = (f32[2048]{0:T(1024)S(1)}, f32[512]{0:T(512)S(1)}, bf16[512,2048]{1,0:T(8,128)(2,1)S(1)}) fusion(f32[64,2048]{1,0:T(8,128)} %get-tuple-element.1336, f32[64,2048]{1,0:T(8,128)S(1)} %get-tuple-element.1334, s32[]{:T(128)S(6)} %select_n.114, f32[2048]{0:T(1024)S(1)} %get-tuple-element.1335, f32[512]{0:T(512)S(1)} %multiply_reduce_fusion.16, ...), kind=kOutput, calls=%fused_computation.78.clone.1 | convolution fusion | flops 828372480 | bytes 2773000 | tf_op jit(solution)/shard_map/while/body/while/body/eval_jaxpr/dot_general | solution.py:74
  257.0 1.8 add_dynamic-update-slice_fusion.10
  258.7 1.8 add_dynamic-update-slice_fusion.11
  260.5 1.1 slice.82
  261.7 0.8 copy.48
  262.5 7.3 %all-to-all-start.6 = ((f32[8,32,256]{2,1,0:T(8,128)}), f32[8,32,256]{2,1,0:T(8,128)S(1)}, u32[]{:S(2)}, u32[]{:S(2)}) async-start(f32[8,32,256]{2,1,0:T(8,128)} %copy.48), calls=%async_computation.6 | async-start | bytes 524288 | tf_op jit(solution)/shard_map/all_to_all | solution.py:45
  270.4 1.6 copy.47
  272.0 4.2 %all-to-all-done.6 = f32[8,32,256]{2,1,0:T(8,128)S(1)} async-done(((f32[8,32,256]{2,1,0:T(8,128)}), f32[8,32,256]{2,1,0:T(8,128)S(1)}, u32[]{:S(2)}, u32[]{:S(2)}) %all-to-all-start.6) | async-done | bytes 262176 | tf_op jit(solution)/shard_map/all_to_all | solution.py:45
  276.2 4.5 %all-to-all-start.5 = ((f32[8,32,1024]{2,1,0:T(8,128)}), f32[8,32,1024]{2,1,0:T(8,128)S(1)}, u32[]{:S(2)}, u32[]{:S(2)}) async-start(f32[8,32,1024]{2,1,0:T(8,128)} %copy.47), calls=%async_computation.5 | async-start | bytes 2097152 | tf_op jit(solution)/shard_map/all_to_all | solution.py:45
  280.7 2.3 collective-permute-start.4
  283.0 1.0 collective-permute-done.4
  284.0 11.7 %all-to-all-done.5 = f32[8,32,1024]{2,1,0:T(8,128)S(1)} async-done(((f32[8,32,1024]{2,1,0:T(8,128)}), f32[8,32,1024]{2,1,0:T(8,128)S(1)}, u32[]{:S(2)}, u32[]{:S(2)}) %all-to-all-start.5) | async-done | bytes 1048608 | tf_op jit(solution)/shard_map/all_to_all | solution.py:45
  296.5 22.0 %all-gather.7.cloned.1.call-done = f32[327680]{0:T(1024)} async-done(((f32[40960]{0:T(1024)}), f32[327680]{0:T(1024)}) %all-gather.7.cloned.1.call-update) | async-done | bytes 1310736 | tf_op jit(solution)/shard_map/all_gather | solution.py:51
  318.5 1.6 reshape.213
  322.0 1.5 multiply_reduce_fusion.6
  323.7 18.0 %all_to_all.43 = f32[32,1,96]{2,1,0:T(1,128)S(1)} all-to-all(f32[32,1,96]{2,1,0:T(1,128)S(1)} %broadcast_in_dim.64), channel_id=1, replica_groups=mesh['blk'=32,'pair'=8] {'blk'}, dimensions={0} | all-to-all | bytes 24576 | tf_op jit(solution)/shard_map/all_to_all | solution.py:22
  341.7 2.9 multiply_subtract_fusion
  (147 shorter events, 27.0 us)
Async XLA Ops:
  8.5 13.5 %all-to-all-start.1 = ((s32[8,2,2]{1,2,0:T(2,128)}), s32[8,2,2]{1,2,0:T(2,128)S(1)}, u32[]{:S(2)}, u32[]{:S(2)}) async-start(s32[8,2,2]{1,2,0:T(2,128)} %broadcast_in_dim.53), calls=%async_computation.1 | async-start | bytes 16384 | tf_op jit(solution)/shard_map/all_to_all | solution.py:22
  16.6 10.0 %copy-start = (f32[32,8192]{1,0:T(8,128)S(1)}, f32[32,8192]{1,0:T(8,128)}, u32[]{:S(2)}) copy-start(f32[32,8192]{1,0:T(8,128)} %param.18) | copy-start | bytes 3145732
  16.6 10.0 %collective-permute-start.1 = (f32[32,2048]{1,0:T(8,128)}, f32[32,2048]{1,0:T(8,128)S(1)}, u32[]{:S(2)}, u32[]{:S(2)}) collective-permute-start(f32[32,2048]{1,0:T(8,128)} %slice.70), channel_id=1, source_target_pairs={{8,0},{16,8},{24,16},{32,24},{40,32},{48,40},{56,48},{64,56},{72,6... | collective-permute-start | bytes 786440 | tf_op jit(solution)/shard_map/ppermute | solution.py:17
  20.7 17.3 %collective-permute-start = (f32[64,2048]{1,0:T(8,128)}, f32[64,2048]{1,0:T(8,128)}, u32[]{:S(2)}, u32[]{:S(2)}) collective-permute-start(f32[64,2048]{1,0:T(8,128)} %slice.88), channel_id=1, source_target_pairs={{8,0},{16,8},{24,16},{32,24},{40,32},{48,40},{56,48},{64,56},{72,6... | collective-permute-start | bytes 1572872 | tf_op jit(solution)/shard_map/ppermute | solution.py:17
  97.1 7.4 %copy-start.3 = (f32[32,10240]{1,0:T(8,128)S(1)}, f32[32,10240]{1,0:T(8,128)}, u32[]{:S(2)}) copy-start(f32[32,10240]{1,0:T(8,128)} %get-tuple-element.778) | copy-start | bytes 3932164
  99.0 11.9 %all-to-all-start.3 = ((f32[8,32,256]{2,1,0:T(8,128)}), f32[8,32,256]{2,1,0:T(8,128)S(1)}, u32[]{:S(2)}, u32[]{:S(2)}) async-start(f32[8,32,256]{2,1,0:T(8,128)} %copy.45), calls=%async_computation.3 | async-start | bytes 524288 | tf_op jit(solution)/shard_map/all_to_all | solution.py:45
  110.9 19.5 %all-to-all-start.2 = ((f32[8,32,1024]{2,1,0:T(8,128)}), f32[8,32,1024]{2,1,0:T(8,128)S(1)}, u32[]{:S(2)}, u32[]{:S(2)}) async-start(f32[8,32,1024]{2,1,0:T(8,128)} %copy.44), calls=%async_computation.2 | async-start | bytes 2097152 | tf_op jit(solution)/shard_map/all_to_all | solution.py:45
  115.4 44.2 %all-gather.5.cloned.1.call-start = ((), (), s32[]{:S(2)}) async-start(), calls=%async_computation.8 | async-start | bytes 1474560 | tf_op jit(solution)/shard_map/all_gather | solution.py:51
  115.5 4.2 %collective-permute-start.2 = (f32[32,256]{1,0:T(8,128)S(1)}, f32[32,256]{1,0:T(8,128)S(1)}, u32[]{:S(2)}, u32[]{:S(2)}) collective-permute-start(f32[32,256]{1,0:T(8,128)S(1)} %reduce_sum.276), channel_id=1, source_target_pairs={{0,8},{8,16},{16,24},{24,32},{32,40},{40,48},{48,56},{56,64},{64,7... | collective-permute-start | bytes 98312 | tf_op jit(solution)/shard_map/ppermute | solution.py:17
  161.3 1.2 copy-start.1
  161.3 1.2 copy-start.11
  162.1 33.6 %copy-start.5 = (f32[32,6144]{1,0:T(8,128)}, f32[32,6144]{1,0:T(8,128)S(1)}, u32[]{:S(2)}) copy-start(f32[32,6144]{1,0:T(8,128)S(1)} %slice.92) | copy-start | bytes 2359300
  162.6 33.1 %copy-start.9 = (f32[32,2048]{1,0:T(8,128)}, f32[32,2048]{1,0:T(8,128)S(1)}, u32[]{:S(2)}) copy-start(f32[32,2048]{1,0:T(8,128)S(1)} %slice_add_fusion.1) | copy-start | bytes 786436
  163.6 18.1 %all-to-all-start = ((f32[32,1,32]{2,1,0:T(1,128)}), f32[32,1,32]{2,1,0:T(1,128)S(1)}, u32[]{:S(2)}, u32[]{:S(2)}) async-start(f32[32,1,32]{2,1,0:T(1,128)} %broadcast_in_dim.52), calls=%async_computation | async-start | bytes 32768 | tf_op jit(solution)/shard_map/all_to_all | solution.py:22
  182.4 12.4 %all-to-all-start.4 = ((f32[32,1,96]{2,1,0:T(1,128)}), f32[32,1,96]{2,1,0:T(1,128)S(1)}, u32[]{:S(2)}, u32[]{:S(2)}) async-start(f32[32,1,96]{2,1,0:T(1,128)} %broadcast_in_dim.63), calls=%async_computation.4 | async-start | bytes 32768 | tf_op jit(solution)/shard_map/all_to_all | solution.py:22
  195.4 0.6 copy-start.13
  195.7 9.7 %copy-start.7 = (f32[32,8192]{1,0:T(8,128)}, f32[32,8192]{1,0:T(8,128)S(1)}, u32[]{:S(2)}) copy-start(f32[32,8192]{1,0:T(8,128)S(1)} %multiply_add_fusion.1) | copy-start | bytes 3145732
  196.0 7.1 %collective-permute-start.3 = (f32[32,2048]{1,0:T(8,128)S(1)}, f32[32,2048]{1,0:T(8,128)S(1)}, u32[]{:S(2)}, u32[]{:S(2)}) collective-permute-start(f32[32,2048]{1,0:T(8,128)S(1)} %slice.93), channel_id=1, source_target_pairs={{8,0},{16,8},{24,16},{32,24},{40,32},{48,40},{56,48},{64,56},{72,6... | collective-permute-start | bytes 786440 | tf_op jit(solution)/shard_map/ppermute | solution.py:17
  260.5 9.2 %copy-start.4 = (f32[32,10240]{1,0:T(8,128)S(1)}, f32[32,10240]{1,0:T(8,128)}, u32[]{:S(2)}) copy-start(f32[32,10240]{1,0:T(8,128)} %get-tuple-element.779) | copy-start | bytes 3932164
  262.5 13.8 %all-to-all-start.6 = ((f32[8,32,256]{2,1,0:T(8,128)}), f32[8,32,256]{2,1,0:T(8,128)S(1)}, u32[]{:S(2)}, u32[]{:S(2)}) async-start(f32[8,32,256]{2,1,0:T(8,128)} %copy.48), calls=%async_computation.6 | async-start | bytes 524288 | tf_op jit(solution)/shard_map/all_to_all | solution.py:45
  276.2 19.5 %all-to-all-start.5 = ((f32[8,32,1024]{2,1,0:T(8,128)}), f32[8,32,1024]{2,1,0:T(8,128)S(1)}, u32[]{:S(2)}, u32[]{:S(2)}) async-start(f32[8,32,1024]{2,1,0:T(8,128)} %copy.47), calls=%async_computation.5 | async-start | bytes 2097152 | tf_op jit(solution)/shard_map/all_to_all | solution.py:45
  280.7 37.8 %all-gather.7.cloned.1.call-start = ((), (), s32[]{:S(2)}) async-start(), calls=%async_computation.9 | async-start | bytes 1474560 | tf_op jit(solution)/shard_map/all_gather | solution.py:51
  280.7 3.3 collective-permute-start.4
  320.2 1.2 copy-start.2
  320.2 1.4 copy-start.6
  320.2 1.8 copy-start.8
  320.2 1.8 copy-start.10
  320.2 1.8 copy-start.12
  320.2 1.8 copy-start.14
  322.0 19.7 %copy-start.15 = (f32[32]{0:T(128)S(1)}, f32[32]{0:T(128)}, u32[]{:S(2)}) copy-start(f32[32]{0:T(128)} %get-tuple-element.948) | copy-start | bytes 388
Sparse Core Ops, SparseCore 0:
  131.4 28.2 all-gather.4
  296.6 21.8 all-gather.6
where the time goes:
time: 353 us; the launch traced here: 351 us
  waiting for transfers between devices  119 us (34%)
  matrix products  86.2 us (24%)
  starting transfers between devices  51.1 us (14%)
  local copies, waits for them, and re-layouts  29.5 us (8%)
  other arithmetic  27.5 us (8%)
  blocking collectives  18 us (5%)
  between operations  15 us (4%)
  loops' own time  5.51 us (2%)
    dot_general x8, matrix products, kernel_tile(): lax.dot_general(left_scaled, right_scaled, (((0,), (0,)), ((), ())), prec...  76.6 us
    all_gather x2, waiting for transfers between devices, one_gather(): lines, at, gathered = (lax.all_gather(vector, axis), 0, [])  50.4 us
    all_to_all x4, waiting for transfers between devices, summed_on_arrival(): lax.all_to_all(parts, axis, split_axis=0, concat_axis=0, tiled=True)  30.8 us
    all_to_all x4, starting transfers between devices, summed_on_arrival(): lax.all_to_all(parts, axis, split_axis=0, concat_axis=0, tiled=True)  21.7 us
    ppermute x5, waiting for transfers between devices, passed_along(): return lax.ppermute(block, axis, route)  20.2 us
    all_to_all x3, starting transfers between devices, copy_for_each(): lax.all_to_all(jnp.broadcast_to(array[None], (count, *array.shape)), axis...  19.8 us
    all_to_all x1, blocking collectives, copy_for_each(): lax.all_to_all(jnp.broadcast_to(array[None], (count, *array.shape)), axis...  18 us
    all_to_all x3, waiting for transfers between devices, copy_for_each(): lax.all_to_all(jnp.broadcast_to(array[None], (count, *array.shape)), axis...  17.1 us
  transfers between devices with their start and end apart: 14, of which 13 were waited for; matrix products, arithmetic and copies ran while one was open for 3% of the time, Pallas kernels for 0%

commit v1 on v0

v1 whole, which is shorter than its diff:
```python
import functools
import math

import jax
import jax.numpy as jnp
from jax import lax
from jax.experimental import pallas as pl
from jax.experimental.pallas import tpu as pltpu
from jax.sharding import PartitionSpec as P

F = 64
R = 32
CHIPS = 4
TORUS = {32: (4, 8), 8: (2, 4), 2: (1, 2)}
LANES = 256
TERMS = 512
MESH = pl.DeviceIdType.MESH

ROOT3 = math.sqrt(3.0)
W = 2.0 * ROOT3 * math.log2(math.e)
SCALE = 2.0**-W / W**4
Q0 = 5.0 * (1.0 + 2.0 * ROOT3) * SCALE
Q1 = -(4.0 * (1.0 + 2.0 * ROOT3) + 10.0 * ROOT3) / W * SCALE
Q2 = 8.0 * ROOT3 / W**2 * SCALE
TINY = 1e-30


def split3(s):
    hi = s.astype(jnp.bfloat16)
    rest = s - hi.astype(jnp.float32)
    mid = rest.astype(jnp.bfloat16)
    lo = (rest - mid.astype(jnp.float32)).astype(jnp.bfloat16)
    return hi, mid, lo


def norm_rows(norms, first):
    n = norms.shape[1]
    hi, mid, lo = split3(norms)
    row = lax.broadcasted_iota(jnp.int32, (8, n), 0)
    base = 0 if first else 3
    ones = (row >= 3 - base) & (row < 6 - base)
    top = jnp.where(row == base, hi.astype(jnp.float32), 0.0)
    top = jnp.where(row == base + 1, mid.astype(jnp.float32), top)
    top = jnp.where(row == base + 2, lo.astype(jnp.float32), top)
    top = jnp.where(ones, 1.0, top)
    return jnp.concatenate([top, jnp.zeros((F - 8, n), jnp.float32)], 0).astype(jnp.bfloat16)


def left_terms(x, inv):
    s = x * inv
    norms = jnp.sum(s * s, axis=0, keepdims=True)
    hi, mid, lo = split3(-2.0 * s)
    return jnp.concatenate([hi, mid], 0).T, jnp.concatenate([lo, norm_rows(norms, False)], 0).T


def right_terms(x, inv):
    s = x * inv
    norms = jnp.sum(s * s, axis=0, keepdims=True)
    hi, mid, lo = split3(s)
    return jnp.concatenate([hi, hi, mid, mid, lo, jnp.zeros_like(lo), hi, norm_rows(norms, True)], 0)


def tile_values(sq, c0, c1, c2):
    y = jnp.maximum(sq, TINY)
    w = y * lax.rsqrt(y)
    u = jnp.maximum(W - w, 0.0)
    u2 = u * u
    return ((c2 * u + c1) * u + c0) * jnp.exp2(u) * (u2 * u2)


def tile_pass(slot, ch, bs, l_ref, r_ref, k_ref, v_ref, p_ref, s_ref, sig, sq_ref, h_ref):
    c0, c1, c2 = sig * Q0, sig * Q1, sig * Q2
    n = bs // ch
    base = slot * bs

    def lanes(j, _):
        cols = pl.ds(pl.multiple_of(j * LANES, LANES), LANES)

        def at(i):
            return pl.ds(pl.multiple_of(base + i * ch, ch), ch)

        def cross(i, buf):
            sq_ref[buf] = jnp.dot(l_ref[at(i), :], r_ref[:, cols], preferred_element_type=jnp.float32)

        def values(i, buf, sums):
            t = tile_values(sq_ref[buf], c0, c1, c2)
            half = t.astype(jnp.bfloat16)
            h_ref[buf] = half
            k_ref[at(i), cols] = half
            return sums + jnp.sum(t.reshape(ch // 8, 8, LANES), axis=0)

        def prod(i, buf, acc):
            return acc + jnp.dot(v_ref[:, at(i)], h_ref[buf], preferred_element_type=jnp.float32)

        acc = jnp.zeros((R, LANES), jnp.float32)
        sums = jnp.zeros((8, LANES), jnp.float32)
        cross(0, 0)
        cross(1, 1)
        sums = values(0, 0, sums)

        def rows(m, carry):
            acc, sums = carry
            i = 2 * m + 1
            cross(i + 1, 0)
            sums = values(i, 1, sums)
            acc = prod(i - 1, 0, acc)
            cross(i + 2, 1)
            sums = values(i + 1, 0, sums)
            acc = prod(i, 1, acc)
            return acc, sums

        acc, sums = lax.fori_loop(0, (n - 2) // 2, rows, (acc, sums))
        sums = values(n - 1, 1, sums)
        acc = prod(n - 2, 0, acc)
        acc = prod(n - 1, 1, acc)
        p_ref[slot, :, cols] = acc
        s_ref[slot, :, cols] = jnp.broadcast_to(jnp.sum(sums, axis=0, keepdims=True), (8, LANES))
        return 0

    lax.fori_loop(0, p_ref.shape[2] // LANES, lanes, 0)


def kernel(
    nx, nz, bs,
    x_hbm, inv_ref, sig_ref, noise_hbm, b_hbm, pairs_ref,
    sol_hbm, res_hbm,
    x_ref, l_ref, r_ref, k_ref, b_ref, bh_ref, q1_ref, qh_ref, q2_ref, v_ref,
    p_ref, s_ref, noise_ref, sq_ref, h_ref, flag_ref, group_ref, st_ref, sx_ref, sz_ref,
    sol_ref, res_ref,
    local_sem, out_sem, halo_send, halo_recv, flag_send, flag_recv, sum_send, sum_recv, part_send, part_recv,
):
    own = bs // 2
    ch = bs // 4
    count = nx * nz
    g = lax.axis_index("blk")
    me = lax.axis_index("pair")
    y, h = me // 2, me % 2
    gx, gz = g // nz, g % nz
    up, down, across = (y + 1) % CHIPS, (y + CHIPS - 1) % CHIPS, (y + 2) % CHIPS
    partner = (g, y * 2 + 1 - h)
    after, before = (g + 1) % count, (g + count - 1) % count
    edge = (y == 0) | (y == CHIPS - 1)
    first = jnp.where(y == 0, 1, y - 1)
    last = jnp.minimum(y + 1, CHIPS - 1)

    def block(i):
        return pl.ds(pl.multiple_of(i * bs, bs), bs)

    def piece(i):
        return pl.ds(pl.multiple_of(i * own, own), own)

    mine = piece(me)

    barrier = pltpu.get_barrier_semaphore()

    def greet(device):
        pl.semaphore_signal(barrier, inc=1, device_id=device, device_id_type=MESH)

    for k in range(1, 8):
        greet((g, (me + k) % 8))
    for k in range(1, nx):
        greet((((gx + k) % nx) * nz + gz, me))
    for k in range(1, nz):
        greet((gx * nz + (gz + k) % nz, me))

    @pl.when(y == CHIPS - 1)
    def _():
        greet((after, h))

    @pl.when(y == 0)
    def _():
        greet((before, (CHIPS - 1) * 2 + h))

    load_x0 = pltpu.make_async_copy(x_hbm.at[:, block(y)], x_ref.at[:, pl.ds(0, bs)], local_sem.at[0])
    load_x1 = pltpu.make_async_copy(x_hbm.at[:, block(first)], x_ref.at[:, pl.ds(bs, bs)], local_sem.at[1])
    load_x2 = pltpu.make_async_copy(x_hbm.at[:, block(last)], x_ref.at[:, pl.ds(2 * bs, bs)], local_sem.at[2])
    load_b = pltpu.make_async_copy(b_hbm, b_ref, local_sem.at[3])
    load_bh = pltpu.make_async_copy(b_hbm.at[:, block(last)], bh_ref, local_sem.at[4])
    load_noise = pltpu.make_async_copy(noise_hbm.at[:, mine], noise_ref, local_sem.at[5])
    load_x0.start()
    load_b.start()
    load_x1.start()
    load_noise.start()

    @pl.when(jnp.logical_not(edge))
    def _():
        load_x2.start()
        load_bh.start()

    row = lax.broadcasted_iota(jnp.int32, (8, 128), 0)
    flags = jnp.zeros((8, 128), jnp.float32)
    for k in range(CHIPS):
        left = g * CHIPS + k
        listed = jnp.float32(0.0)
        for s in range(2):
            hit = (pairs_ref[s, 0] == left) & (pairs_ref[s, 1] == left + 1)
            listed = listed + jnp.where(hit, 1.0, 0.0)
        flags = jnp.where(row == k, listed, flags)
    flag_ref[me] = flags

    inv = jnp.tile(inv_ref[...], (1, ch // 128))

    def prepare(slot):
        def part(i, _):
            at = pl.ds(pl.multiple_of(slot * bs + i * ch, ch), ch)
            a, c = left_terms(x_ref[:, at], inv)
            l_ref[at, 0:128] = a
            l_ref[at, 128:256] = a
            l_ref[at, 256:384] = a
            l_ref[at, 384:512] = c
            return 0

        lax.fori_loop(0, bs // ch, part, 0)

    load_x0.wait()
    prepare(0)
    for i in range(own // ch):
        at = pl.ds(pl.multiple_of(h * own + i * ch, ch), ch)
        r_ref[:, i * ch : (i + 1) * ch] = right_terms(x_ref[:, at], inv)
    load_b.wait()
    v_ref[:, 0:bs] = b_ref[:, block(y)].astype(jnp.bfloat16)

    pl.semaphore_wait(barrier, 5 + nx + nz + jnp.where(edge, 1, 0))

    half = pl.ds(pl.multiple_of(h * own, own), own)
    half_x = pl.ds(pl.multiple_of(2 * bs + h * own, own), own)
    other = pl.ds(pl.multiple_of((1 - h) * own, own), own)
    other_x = pl.ds(pl.multiple_of(2 * bs + (1 - h) * own, own), own)

    def halo_x(device, src):
        return pltpu.make_async_remote_copy(
            x_hbm.at[:, piece(src)], x_ref.at[:, half_x], halo_send.at[0], halo_recv.at[h],
            device_id=device, device_id_type=MESH)

    def halo_b(device, src):
        return pltpu.make_async_remote_copy(
            b_hbm.at[:, piece(src)], bh_ref.at[:, half], halo_send.at[1], halo_recv.at[2 + h],
            device_id=device, device_id_type=MESH)

    def halo_q(device):
        return pltpu.make_async_remote_copy(
            q1_ref.at[:, mine], qh_ref.at[:, half], halo_send.at[2], halo_recv.at[4 + h],
            device_id=device, device_id_type=MESH)

    def pass_on(ref, at, k, sem):
        return pltpu.make_async_remote_copy(
            ref.at[:, at], ref.at[:, at], halo_send.at[3 + k], halo_recv.at[2 * k + sem],
            device_id=partner, device_id_type=MESH)

    forward_dev = (after, h)
    backward_dev = (before, (CHIPS - 1) * 2 + h)

    @pl.when(y == CHIPS - 1)
    def _():
        halo_x(forward_dev, me).start()
        halo_b(forward_dev, me).start()

    @pl.when(y == 0)
    def _():
        halo_x(backward_dev, me).start()
        halo_b(backward_dev, me).start()

    def flag_copy(k):
        return pltpu.make_async_remote_copy(
            flag_ref.at[me], flag_ref.at[me], flag_send.at[k], flag_recv.at[k],
            device_id=(g, (me + k) % 8), device_id_type=MESH)

    def flag_arrival(k):
        src = (me + 8 - k) % 8
        return pltpu.make_async_remote_copy(
            flag_ref.at[src], flag_ref.at[src], flag_send.at[k], flag_recv.at[k],
            device_id=(g, src), device_id_type=MESH)

    for k in range(1, 8):
        flag_copy(k).start()

    sig = sig_ref[0]
    passes = functools.partial(
        tile_pass, l_ref=l_ref, r_ref=r_ref, k_ref=k_ref, v_ref=v_ref, p_ref=p_ref, s_ref=s_ref,
        sig=sig, sq_ref=sq_ref, h_ref=h_ref)

    passes(0, ch, bs)

    for k in range(1, 8):
        flag_arrival(k).wait_recv()
    total_flags = flag_ref[0]
    for k in range(1, 8):
        total_flags = total_flags + flag_ref[k]
    group_ref[0] = total_flags
    group_copy = pltpu.make_async_remote_copy(
        group_ref.at[0], group_ref.at[1], flag_send.at[0], flag_recv.at[0],
        device_id=forward_dev, device_id_type=MESH)

    @pl.when(y == CHIPS - 1)
    def _():
        group_copy.start()

    load_x1.wait()
    prepare(1)
    v_ref[:, bs : 2 * bs] = b_ref[:, block(first)].astype(jnp.bfloat16)
    passes(1, ch, bs)

    @pl.when(jnp.logical_not(edge))
    def _():
        load_x2.wait()
        load_bh.wait()

    @pl.when(edge)
    def _():
        pass_on(x_ref, half_x, 0, h).wait_recv()
        pass_on(x_ref, half_x, 0, h).start()
        pass_on(bh_ref, half, 1, h).wait_recv()
        pass_on(bh_ref, half, 1, h).start()
        pass_on(x_ref, other_x, 0, 1 - h).wait_recv()
        pass_on(bh_ref, other, 1, 1 - h).wait_recv()

    prepare(2)
    v_ref[:, 2 * bs : 3 * bs] = bh_ref[...].astype(jnp.bfloat16)
    passes(2, ch, bs)

    @pl.when(y == 0)
    def _():
        group_copy.wait_recv()

    load_noise.wait()
    flag_first = group_ref[0, pl.ds(jnp.maximum(y - 1, 0), 1), :]

    @pl.when(y > 0)
    def _():
        group_ref[2, 0:1, :] = group_ref[0, pl.ds(y, 1), :]

    @pl.when(y == 0)
    def _():
        group_ref[2, 0:1, :] = group_ref[1, CHIPS - 1 : CHIPS, :]

    flag_last = group_ref[2, 0:1, :]
    flag_first = jnp.tile(flag_first, (1, own // 128))
    flag_last = jnp.tile(flag_last, (1, own // 128))
    diagonal = noise_ref[...] + flag_first * s_ref[1, 0:1, :] + flag_last * s_ref[2, 0:1, :]

    def image(vec):
        return diagonal * vec + (p_ref[0] + flag_first * p_ref[1] + flag_last * p_ref[2])

    lane = lax.broadcasted_iota(jnp.int32, (R, 128), 1)

    def set_stats(t, arrays):
        stats = jnp.zeros((R, 128), jnp.float32)
        for k, a in enumerate(arrays):
            stats = jnp.where(lane == k, jnp.sum(a, axis=1, keepdims=True), stats)
        padded = jnp.concatenate([stats, jnp.zeros((128 - R, 128), jnp.float32)], 0)
        st_ref[t, me] = padded.T[0:8]

    def sum_copies(t, ref, stage, n, place, device_of):
        def send(k):
            return pltpu.make_async_remote_copy(
                ref.at[t, place], ref.at[t, place], sum_send.at[t, stage, k], sum_recv.at[t, stage, k],
                device_id=device_of((place + k) % n), device_id_type=MESH)

        def arrival(k):
            src = (place + n - k) % n
            return pltpu.make_async_remote_copy(
                ref.at[t, src], ref.at[t, src], sum_send.at[t, stage, k], sum_recv.at[t, stage, k],
                device_id=device_of(src), device_id_type=MESH)

        def start():
            for k in range(1, n):
                send(k).start()

        def finish():
            for k in range(1, n):
                arrival(k).wait_recv()
            total = ref[t, 0]
            for k in range(1, n):
                total = total + ref[t, k]
            return total

        def drain():
            for k in range(1, n):
                send(k).wait_send()

        return start, finish, drain

    def stages(t):
        return (
            sum_copies(t, st_ref, 0, 8, me, lambda p: (g, p)),
            sum_copies(t, sx_ref, 1, nx, gx, lambda p: (p * nz + gz, me)),
            sum_copies(t, sz_ref, 2, nz, gz, lambda p: (gx * nz + p, me)),
        )

    def part_copy(t, ref, which, k, device):
        return pltpu.make_async_remote_copy(
            ref.at[:, piece(which)], ref.at[:, piece(which)], part_send.at[t, k], part_recv.at[t, which],
            device_id=device, device_id_type=MESH)

    def parts(t, ref):
        to_up, to_down = (g, up * 2 + h), (g, down * 2 + h)
        sends = [
            part_copy(t, ref, me, 0, to_up),
            part_copy(t, ref, me, 1, to_down),
            part_copy(t, ref, me, 2, partner),
            part_copy(t, ref, down * 2 + h, 3, partner),
            part_copy(t, ref, up * 2 + h, 4, partner),
            part_copy(t, ref, across * 2 + h, 5, partner),
        ]
        relay_up = part_copy(t, ref, down * 2 + h, 6, to_up)
        relay_down = part_copy(t, ref, up * 2 + h, 6, to_down)

        def arrived(which):
            part_copy(t, ref, which, 0, partner).wait_recv()

        def begin():
            for s in sends[:3]:
                s.start()

        def relay():
            arrived(down * 2 + h)

            @pl.when(h == 0)
            def _():
                relay_up.start()

            sends[3].start()
            arrived(up * 2 + h)

            @pl.when(h == 1)
            def _():
                relay_down.start()

            sends[4].start()

        def near():
            arrived(y * 2 + 1 - h)
            arrived(down * 2 + 1 - h)
            arrived(up * 2 + 1 - h)

        def far():
            arrived(across * 2 + h)
            sends[5].start()
            arrived(across * 2 + 1 - h)

        def drain():
            for s in sends:
                s.wait_send()
            relay_up.wait_send()

        return begin, relay, near, far, drain

    b_own = b_ref[:, mine]
    q_own = image(b_own)
    q1_ref[:, mine] = q_own
    set_stats(0, (b_own * b_own, b_own * q_own, q_own * q_own))

    (a_start, a_finish, a_drain), (x_start, x_finish, x_drain), (z_start, z_finish, z_drain) = stages(0)
    begin, relay, near, far, drain = parts(0, q1_ref)
    a_start()
    begin()

    @pl.when(y == CHIPS - 1)
    def _():
        halo_q(forward_dev).start()

    @pl.when(y == 0)
    def _():
        halo_q(backward_dev).start()

    sx_ref[0, gx] = a_finish()
    x_start()
    sz_ref[0, gz] = x_finish()
    z_start()
    relay()

    @pl.when(edge)
    def _():
        pass_on(qh_ref, half, 2, h).wait_recv()
        pass_on(qh_ref, half, 2, h).start()

    total = z_finish()
    norm, curve, square = total[0:1], total[1:2], total[2:3]
    step1 = norm / curve
    norm2 = norm - 2.0 * step1 * curve + step1 * step1 * square
    ratio = norm2 / norm

    def as_columns(rows):
        stacked = jnp.zeros((8, 128), jnp.float32)
        for k, a in enumerate(rows):
            stacked = jnp.where(row == k, a, stacked)
        turned = jnp.concatenate([stacked, jnp.zeros((120, 128), jnp.float32)], 0).T
        return [turned[0:R, k : k + 1] for k in range(len(rows))]

    step1_col, ratio_col = as_columns((step1, ratio))
    near()

    @pl.when(edge)
    def _():
        pass_on(qh_ref, other, 2, 1 - h).wait_recv()

    @pl.when(jnp.logical_not(edge))
    def _():
        qh_ref[...] = q1_ref[:, block(last)]

    def next_direction(b, q):
        return (b - step1_col * q) + ratio_col * b

    v_ref[:, 0:bs] = next_direction(b_ref[:, block(y)], q1_ref[:, block(y)]).astype(jnp.bfloat16)
    v_ref[:, bs : 2 * bs] = next_direction(b_ref[:, block(first)], q1_ref[:, block(first)]).astype(jnp.bfloat16)
    v_ref[:, 2 * bs : 3 * bs] = next_direction(bh_ref[...], qh_ref[...]).astype(jnp.bfloat16)

    def lanes(j, _):
        cols = pl.ds(pl.multiple_of(j * LANES, LANES), LANES)
        for slot in range(3):
            at = pl.ds(slot * bs, bs)
            p_ref[slot, :, cols] = jnp.dot(v_ref[:, at], k_ref[at, cols], preferred_element_type=jnp.float32)
        return 0

    lax.fori_loop(0, own // LANES, lanes, 0)
    d_own = next_direction(b_own, q1_ref[:, mine])
    q2_own = image(d_own)
    q2_ref[:, mine] = q2_own
    set_stats(1, (d_own * q2_own,))
    (a2_start, a2_finish, a2_drain), (x2_start, x2_finish, x2_drain), (z2_start, z2_finish, z2_drain) = stages(1)
    begin2, relay2, near2, far2, drain2 = parts(1, q2_ref)
    a2_start()
    begin2()
    far()
    sx_ref[1, gx] = a2_finish()
    x2_start()
    sz_ref[1, gz] = x2_finish()
    z2_start()
    relay2()
    far2()
    total2 = z2_finish()
    (step2_col,) = as_columns((norm2 / total2[0:1],))
    near2()

    outs = []
    for i in range(CHIPS):
        at = pl.ds(i * bs, bs)
        b = b_ref[:, at]
        r1 = b - step1_col * q1_ref[:, at]
        d2 = r1 + ratio_col * b
        sol_ref[:, at] = step1_col * b + step2_col * d2
        res_ref[:, at] = r1 - step2_col * q2_ref[:, at]
        outs.append(pltpu.make_async_copy(sol_ref.at[:, at], sol_hbm.at[:, at], out_sem.at[2 * i]))
        outs.append(pltpu.make_async_copy(res_ref.at[:, at], res_hbm.at[:, at], out_sem.at[2 * i + 1]))
        outs[-2].start()
        outs[-1].start()

    for k in range(1, 8):
        flag_copy(k).wait_send()
    for wait in (a_drain, x_drain, z_drain, drain, a2_drain, x2_drain, z2_drain, drain2):
        wait()

    @pl.when(edge)
    def _():
        halo_x(forward_dev, me).wait_send()
        halo_b(forward_dev, me).wait_send()
        halo_q(forward_dev).wait_send()
        pass_on(x_ref, half_x, 0, h).wait_send()
        pass_on(bh_ref, half, 1, h).wait_send()
        pass_on(qh_ref, half, 2, h).wait_send()

    @pl.when(y == CHIPS - 1)
    def _():
        group_copy.wait_send()

    for o in outs:
        o.wait()


def body(features, inv_scale, signal, noise_var, right_side, block_pairs):
    local = features.shape[1]
    bs = local // CHIPS
    own = bs // 2
    nx, nz = TORUS[lax.axis_size("blk")]
    inv = jnp.broadcast_to((inv_scale * (W / 16.0))[:, None], (F, 128))
    vmem = pltpu.VMEM
    dma = pltpu.SemaphoreType.DMA
    f32, bf16 = jnp.float32, jnp.bfloat16
    hbm = pl.BlockSpec(memory_space=pl.ANY)
    smem = pl.BlockSpec(memory_space=pltpu.SMEM)
    shape = jax.ShapeDtypeStruct(right_side.shape, f32)
    return pl.pallas_call(
        functools.partial(kernel, nx, nz, bs),
        name="conjugate_gradients",
        out_shape=(shape, shape),
        in_specs=[hbm, pl.BlockSpec(memory_space=pltpu.VMEM), smem, hbm, hbm, smem],
        out_specs=(hbm, hbm),
        scratch_shapes=[
            vmem((F, 3 * bs), f32),
            vmem((3 * bs, TERMS), bf16),
            vmem((TERMS, own), bf16),
            vmem((3 * bs, own), bf16),
            vmem((R, local), f32),
            vmem((R, bs), f32),
            vmem((R, local), f32),
            vmem((R, bs), f32),
            vmem((R, local), f32),
            vmem((R, 3 * bs), bf16),
            vmem((3, R, own), f32),
            vmem((3, 8, own), f32),
            vmem((1, own), f32),
            vmem((2, bs // 4, LANES), f32),
            vmem((2, bs // 4, LANES), bf16),
            vmem((8, 8, 128), f32),
            vmem((3, 8, 128), f32),
            vmem((2, 8, 8, 128), f32),
            vmem((2, nx, 8, 128), f32),
            vmem((2, nz, 8, 128), f32),
            vmem((R, local), f32),
            vmem((R, local), f32),
            dma((6,)),
            dma((8,)),
            dma((6,)),
            dma((6,)),
            dma((8,)),
            dma((8,)),
            dma((2, 3, 8)),
            dma((2, 3, 8)),
            dma((2, 7)),
            dma((2, 8)),
        ],
        compiler_params=pltpu.CompilerParams(
            collective_id=0, has_side_effects=True, vmem_limit_bytes=60 * 1024 * 1024
        ),
    )(features, inv, signal, noise_var.reshape(1, -1), right_side, block_pairs)


def solution(mesh):
    placed = (P(None, "blk"), P(), P(), P("blk"), P(None, "blk"), P(("blk", "pair"), None))
    return jax.shard_map(
        body,
        mesh=mesh,
        in_specs=placed,
        out_specs=(P(None, "blk"), P(None, "blk")),
        check_vma=False,
    )
```

time: 353 us -> 70.2 us (0.20)
  waiting for transfers between devices: 119 us -> 0 us
  matrix products: 86.2 us -> 0 us
  Pallas kernels: 0 us -> 63.5 us
  starting transfers between devices: 51.1 us -> 0 us
  other arithmetic: 27.5 us -> 0.66 us
  local copies, waits for them, and re-layouts: 29.5 us -> 4.02 us
  blocking collectives: 18 us -> 0 us
  between operations: 15 us -> 1.29 us
  loops' own time: 5.51 us -> 0 us
    dot_general x24 -> x0, matrix products: 86.2 us -> none  [the longest x8 76.6 us: kernel_tile(): lax.dot_general(left_scaled, right_scaled, (((0,), (0,)), ((), ())), prec...]
    pallas_call x0 -> x1, Pallas kernels: none -> 63.5 us  [body(): pl.pallas_call(functools.partial(kernel, nx, nz, bs), name='conjugate_gra...]
    all_gather x2 -> x0, waiting for transfers between devices: 50.4 us -> none  [one_gather(): lines, at, gathered = (lax.all_gather(vector, axis), 0, [])]
    all_to_all x7 -> x0, waiting for transfers between devices: 47.9 us -> none  [the longest x4 30.8 us: summed_on_arrival(): lax.all_to_all(parts, axis, split_axis=0, concat_axis=0, tiled=True)]
    all_to_all x7 -> x0, starting transfers between devices: 41.5 us -> none  [the longest x4 21.7 us: summed_on_arrival(): lax.all_to_all(parts, axis, split_axis=0, concat_axis=0, tiled=True)]
    ppermute x5 -> x0, waiting for transfers between devices: 20.2 us -> none  [passed_along(): return lax.ppermute(block, axis, route)]
    all_to_all x1 -> x0, blocking collectives: 18 us -> none  [copy_for_each(): lax.all_to_all(jnp.broadcast_to(array[None], (count, *array.shape)), axis...]
    ppermute x5 -> x0, starting transfers between devices: 9.61 us -> none  [passed_along(): return lax.ppermute(block, axis, route)]
  transfers between devices with their start and end apart: 14 -> 0, of which waited for: 13 -> 0; matrix products, arithmetic and copies ran while one was open for 3% -> 0% of each run, Pallas kernels for 0% -> 0%
where the time goes in v1:
time: 70.2 us; the launch traced here: 69.5 us
  Pallas kernels  63.5 us (90%)
  local copies, waits for them, and re-layouts  4.02 us (6%)
  between operations  1.29 us (2%)
    pallas_call x1, Pallas kernels, body(): pl.pallas_call(functools.partial(kernel, nx, nz, bs), name='conjugate_gra...  63.5 us
    unnamed x4, local copies, waits for them, and re-layouts  3.32 us

profile of v1, /device:TPU:1, one launch (start us, length us, event | category | flops | bytes accessed | tf_op | source)
XLA Modules:
  0.0 69.5 jit_solution(15753645494321106743)
XLA Ops:
  1.3 0.7 broadcast_multiply_fusion
  1.9 0.7 broadcast_in_dim.2.inv_ref
  2.6 63.5 %conjugate_gradients.1 = (f32[32,8192]{1,0:T(8,128)}, f32[32,8192]{1,0:T(8,128)}) custom-call(f32[64,8192]{1,0:T(8,128)} %x_hbm.1, f32[64,128]{1,0:T(8,128)} %broadcast_in_dim.2.inv_ref, f32[1]{0:T(128)S(6)} %copy.10.sig_ref, f32[1,8192]{1,0:T(1,128)} %bitcast.1, f32[32,8192]{1,0:T(8,128)} %b_hbm.1, s32[2,2]{1,0:T(2,128)} %pairs_ref.1), custom_call_target="tpu_custom_call" | custom-call | tf_op jit(solution)/shard_map/conjugate_gradients/pallas_call | solution.py:582
  66.1 0.0 copy-start
  66.2 2.4 %copy.11 = f32[32,8192]{1,0:T(8,128)} copy(f32[32,8192]{1,0:T(8,128)} %get-tuple-element.4) | data formatting | bytes 2097152
  68.5 0.0 copy-done
  68.5 1.0 %copy.12 = f32[32,8192]{1,0:T(8,128)} copy(f32[32,8192]{1,0:T(8,128)S(1)} %copy-done) | data formatting | bytes 2097152
Async XLA Ops:
  66.1 2.4 %copy-start = (f32[32,8192]{1,0:T(8,128)S(1)}, f32[32,8192]{1,0:T(8,128)}, u32[]{:S(2)}) copy-start(f32[32,8192]{1,0:T(8,128)} %get-tuple-element.5) | copy-start | bytes 3145732

commit v2 on v1

--- a/solution.py
+++ b/solution.py
@@ -68,7 +68,7 @@
     return ((c2 * u + c1) * u + c0) * jnp.exp2(u) * (u2 * u2)
 
 
-def tile_pass(slot, ch, bs, l_ref, r_ref, k_ref, v_ref, p_ref, s_ref, sig, sq_ref, h_ref):
+def tile_pass(slot, ch, bs, l_ref, r_ref, k_ref, v_ref, p_ref, s_ref, sig, sq_ref, h_ref, after=None):
     c0, c1, c2 = sig * Q0, sig * Q1, sig * Q2
     n = bs // ch
     base = slot * bs
@@ -115,6 +115,8 @@
         acc = prod(n - 1, 1, acc)
         p_ref[slot, :, cols] = acc
         s_ref[slot, :, cols] = jnp.broadcast_to(jnp.sum(sums, axis=0, keepdims=True), (8, LANES))
+        if after is not None:
+            after(j, cols)
         return 0
 
     lax.fori_loop(0, p_ref.shape[2] // LANES, lanes, 0)
@@ -123,11 +125,11 @@
 def kernel(
     nx, nz, bs,
     x_hbm, inv_ref, sig_ref, noise_hbm, b_hbm, pairs_ref,
-    sol_hbm, res_hbm,
+    q1_hbm, q2_hbm, coef_ref,
     x_ref, l_ref, r_ref, k_ref, b_ref, bh_ref, q1_ref, qh_ref, q2_ref, v_ref,
     p_ref, s_ref, noise_ref, sq_ref, h_ref, flag_ref, group_ref, st_ref, sx_ref, sz_ref,
-    sol_ref, res_ref,
-    local_sem, out_sem, halo_send, halo_recv, flag_send, flag_recv, sum_send, sum_recv, part_send, part_recv,
+    diag_ref,
+    local_sem, out_sem, halo_send, halo_recv, edge_send, edge_recv, flag_send, flag_recv, sum_send, sum_recv, part_send, part_recv,
 ):
     own = bs // 2
     ch = bs // 4
@@ -198,7 +200,9 @@
         flags = jnp.where(row == k, listed, flags)
     flag_ref[me] = flags
 
-    inv = jnp.tile(inv_ref[...], (1, ch // 128))
+    scale = inv_ref[...] * (W / 16.0)
+    scale = jnp.broadcast_to(jnp.concatenate([scale, scale], 1), (128, 2 * F)).T[0:F]
+    inv = jnp.tile(scale, (1, ch // 128))
 
     def prepare(slot):
         def part(i, _):
@@ -219,6 +223,9 @@
         r_ref[:, i * ch : (i + 1) * ch] = right_terms(x_ref[:, at], inv)
     load_b.wait()
     v_ref[:, 0:bs] = b_ref[:, block(y)].astype(jnp.bfloat16)
+    v_ref[:, bs : 2 * bs] = b_ref[:, block(first)].astype(jnp.bfloat16)
+    load_x1.wait()
+    prepare(1)
 
     pl.semaphore_wait(barrier, 5 + nx + nz + jnp.where(edge, 1, 0))
 
@@ -237,14 +244,24 @@
             b_hbm.at[:, piece(src)], bh_ref.at[:, half], halo_send.at[1], halo_recv.at[2 + h],
             device_id=device, device_id_type=MESH)
 
-    def halo_q(device):
-        return pltpu.make_async_remote_copy(
-            q1_ref.at[:, mine], qh_ref.at[:, half], halo_send.at[2], halo_recv.at[4 + h],
+    chunks = own // LANES
+
+    def slab(i, c):
+        return pl.ds(pl.multiple_of(i * own + c * LANES, LANES), LANES)
+
+    def edge_q(device, c):
+        return pltpu.make_async_remote_copy(
+            q1_ref.at[:, slab(me, c)], qh_ref.at[:, slab(h, c)], edge_send.at[0, c], edge_recv.at[h, c],
             device_id=device, device_id_type=MESH)
 
+    def edge_on(side, c):
+        return pltpu.make_async_remote_copy(
+            qh_ref.at[:, slab(side, c)], qh_ref.at[:, slab(side, c)], edge_send.at[1, c], edge_recv.at[side, c],
+            device_id=partner, device_id_type=MESH)
+
     def pass_on(ref, at, k, sem):
         return pltpu.make_async_remote_copy(
-            ref.at[:, at], ref.at[:, at], halo_send.at[3 + k], halo_recv.at[2 * k + sem],
+            ref.at[:, at], ref.at[:, at], halo_send.at[2 + k], halo_recv.at[2 * k + sem],
             device_id=partner, device_id_type=MESH)
 
     forward_dev = (after, h)
@@ -295,9 +312,6 @@
     def _():
         group_copy.start()
 
-    load_x1.wait()
-    prepare(1)
-    v_ref[:, bs : 2 * bs] = b_ref[:, block(first)].astype(jnp.bfloat16)
     passes(1, ch, bs)
 
     @pl.when(jnp.logical_not(edge))
@@ -316,30 +330,50 @@
 
     prepare(2)
     v_ref[:, 2 * bs : 3 * bs] = bh_ref[...].astype(jnp.bfloat16)
-    passes(2, ch, bs)
+    load_noise.wait()
 
     @pl.when(y == 0)
     def _():
         group_copy.wait_recv()
-
-    load_noise.wait()
-    flag_first = group_ref[0, pl.ds(jnp.maximum(y - 1, 0), 1), :]
+        group_ref[2, 0:1, :] = group_ref[1, CHIPS - 1 : CHIPS, :]
 
     @pl.when(y > 0)
     def _():
         group_ref[2, 0:1, :] = group_ref[0, pl.ds(y, 1), :]
 
-    @pl.when(y == 0)
-    def _():
-        group_ref[2, 0:1, :] = group_ref[1, CHIPS - 1 : CHIPS, :]
-
-    flag_last = group_ref[2, 0:1, :]
-    flag_first = jnp.tile(flag_first, (1, own // 128))
-    flag_last = jnp.tile(flag_last, (1, own // 128))
-    diagonal = noise_ref[...] + flag_first * s_ref[1, 0:1, :] + flag_last * s_ref[2, 0:1, :]
-
-    def image(vec):
-        return diagonal * vec + (p_ref[0] + flag_first * p_ref[1] + flag_last * p_ref[2])
+    flag_first = jnp.tile(group_ref[0, pl.ds(jnp.maximum(y - 1, 0), 1), :], (1, LANES // 128))
+    flag_last = jnp.tile(group_ref[2, 0:1, :], (1, LANES // 128))
+
+    to_up, to_down = (g, up * 2 + h), (g, down * 2 + h)
+
+    def part_copy(t, ref, which, c, k, device):
+        return pltpu.make_async_remote_copy(
+            ref.at[:, slab(which, c)], ref.at[:, slab(which, c)], part_send.at[t, k, c], part_recv.at[t, which, c],
+            device_id=device, device_id_type=MESH)
+
+    def hand_out(t, ref, c):
+        part_copy(t, ref, me, c, 0, to_up).start()
+        part_copy(t, ref, me, c, 1, to_down).start()
+        part_copy(t, ref, me, c, 2, partner).start()
+
+    def image(cols, vec):
+        return diag_ref[:, cols] * vec + (p_ref[0, :, cols] + flag_first * p_ref[1, :, cols] + flag_last * p_ref[2, :, cols])
+
+    def first_image(j, cols):
+        at = slab(me, j)
+        diag_ref[:, cols] = noise_ref[:, cols] + flag_first * s_ref[1, 0:1, cols] + flag_last * s_ref[2, 0:1, cols]
+        q1_ref[:, at] = image(cols, b_ref[:, at])
+        hand_out(0, q1_ref, j)
+
+        @pl.when(y == CHIPS - 1)
+        def _():
+            edge_q(forward_dev, j).start()
+
+        @pl.when(y == 0)
+        def _():
+            edge_q(backward_dev, j).start()
+
+    passes(2, ch, bs, after=first_image)
 
     lane = lax.broadcasted_iota(jnp.int32, (R, 128), 1)
 
@@ -387,92 +421,68 @@
             sum_copies(t, sz_ref, 2, nz, gz, lambda p: (gx * nz + p, me)),
         )
 
-    def part_copy(t, ref, which, k, device):
-        return pltpu.make_async_remote_copy(
-            ref.at[:, piece(which)], ref.at[:, piece(which)], part_send.at[t, k], part_recv.at[t, which],
-            device_id=device, device_id_type=MESH)
-
     def parts(t, ref):
-        to_up, to_down = (g, up * 2 + h), (g, down * 2 + h)
-        sends = [
-            part_copy(t, ref, me, 0, to_up),
-            part_copy(t, ref, me, 1, to_down),
-            part_copy(t, ref, me, 2, partner),
-            part_copy(t, ref, down * 2 + h, 3, partner),
-            part_copy(t, ref, up * 2 + h, 4, partner),
-            part_copy(t, ref, across * 2 + h, 5, partner),
-        ]
-        relay_up = part_copy(t, ref, down * 2 + h, 6, to_up)
-        relay_down = part_copy(t, ref, up * 2 + h, 6, to_down)
-
-        def arrived(which):
-            part_copy(t, ref, which, 0, partner).wait_recv()
-
-        def begin():
-            for s in sends[:3]:
-                s.start()
+        def arrived(which, c):
+            part_copy(t, ref, which, c, 0, partner).wait_recv()
 
         def relay():
-            arrived(down * 2 + h)
-
-            @pl.when(h == 0)
-            def _():
-                relay_up.start()
-
-            sends[3].start()
-            arrived(up * 2 + h)
-
-            @pl.when(h == 1)
-            def _():
-                relay_down.start()
-
-            sends[4].start()
+            for c in range(chunks):
+                arrived(down * 2 + h, c)
+
+                @pl.when(h == 0)
+                def _():
+                    part_copy(t, ref, down * 2 + h, c, 6, to_up).start()
+
+                part_copy(t, ref, down * 2 + h, c, 3, partner).start()
+                arrived(up * 2 + h, c)
+
+                @pl.when(h == 1)
+                def _():
+                    part_copy(t, ref, up * 2 + h, c, 6, to_down).start()
+
+                part_copy(t, ref, up * 2 + h, c, 4, partner).start()
 
         def near():
-            arrived(y * 2 + 1 - h)
-            arrived(down * 2 + 1 - h)
-            arrived(up * 2 + 1 - h)
+            for c in range(chunks):
+                arrived(y * 2 + 1 - h, c)
+                arrived(down * 2 + 1 - h, c)
+                arrived(up * 2 + 1 - h, c)
+
+        def far_on():
+            for c in range(chunks):
+                arrived(across * 2 + h, c)
+                part_copy(t, ref, across * 2 + h, c, 5, partner).start()
 
         def far():
-            arrived(across * 2 + h)
-            sends[5].start()
-            arrived(across * 2 + 1 - h)
+            for c in range(chunks):
+                arrived(across * 2 + 1 - h, c)
 
         def drain():
-            for s in sends:
-                s.wait_send()
-            relay_up.wait_send()
-
-        return begin, relay, near, far, drain
+            for c in range(chunks):
+                for k in range(7):
+                    part_copy(t, ref, me, c, k, partner).wait_send()
+
+        return relay, near, far_on, far, drain
 
     b_own = b_ref[:, mine]
-    q_own = image(b_own)
-    q1_ref[:, mine] = q_own
+    q_own = q1_ref[:, mine]
     set_stats(0, (b_own * b_own, b_own * q_own, q_own * q_own))
-
     (a_start, a_finish, a_drain), (x_start, x_finish, x_drain), (z_start, z_finish, z_drain) = stages(0)
-    begin, relay, near, far, drain = parts(0, q1_ref)
+    relay, near, far_on, far, drain = parts(0, q1_ref)
     a_start()
-    begin()
-
-    @pl.when(y == CHIPS - 1)
-    def _():
-        halo_q(forward_dev).start()
-
-    @pl.when(y == 0)
-    def _():
-        halo_q(backward_dev).start()
-
     sx_ref[0, gx] = a_finish()
     x_start()
+    relay()
+
+    @pl.when(edge)
+    def _():
+        for c in range(chunks):
+            edge_on(h, c).wait_recv()
+            edge_on(h, c).start()
+
     sz_ref[0, gz] = x_finish()
     z_start()
-    relay()
-
-    @pl.when(edge)
-    def _():
-        pass_on(qh_ref, half, 2, h).wait_recv()
-        pass_on(qh_ref, half, 2, h).start()
+    far_on()
 
     total = z_finish()
     norm, curve, square = total[0:1], total[1:2], total[2:3]
@@ -492,7 +502,8 @@
 
     @pl.when(edge)
     def _():
-        pass_on(qh_ref, other, 2, 1 - h).wait_recv()
+        for c in range(chunks):
+            edge_on(1 - h, c).wait_recv()
 
     @pl.when(jnp.logical_not(edge))
     def _():
@@ -508,42 +519,35 @@
     def lanes(j, _):
         cols = pl.ds(pl.multiple_of(j * LANES, LANES), LANES)
         for slot in range(3):
-            at = pl.ds(slot * bs, bs)
-            p_ref[slot, :, cols] = jnp.dot(v_ref[:, at], k_ref[at, cols], preferred_element_type=jnp.float32)
+            rows = pl.ds(slot * bs, bs)
+            p_ref[slot, :, cols] = jnp.dot(v_ref[:, rows], k_ref[rows, cols], preferred_element_type=jnp.float32)
+        at = slab(me, j)
+        q2_ref[:, at] = image(cols, next_direction(b_ref[:, at], q1_ref[:, at]))
+        hand_out(1, q2_ref, j)
         return 0
 
-    lax.fori_loop(0, own // LANES, lanes, 0)
+    lax.fori_loop(0, chunks, lanes, 0)
     d_own = next_direction(b_own, q1_ref[:, mine])
-    q2_own = image(d_own)
-    q2_ref[:, mine] = q2_own
-    set_stats(1, (d_own * q2_own,))
+    set_stats(1, (d_own * q2_ref[:, mine],))
     (a2_start, a2_finish, a2_drain), (x2_start, x2_finish, x2_drain), (z2_start, z2_finish, z2_drain) = stages(1)
-    begin2, relay2, near2, far2, drain2 = parts(1, q2_ref)
+    relay2, near2, far_on2, far2, drain2 = parts(1, q2_ref)
     a2_start()
-    begin2()
     far()
+    q1_out = pltpu.make_async_copy(q1_ref, q1_hbm, out_sem.at[0])
+    q1_out.start()
     sx_ref[1, gx] = a2_finish()
     x2_start()
+    relay2()
     sz_ref[1, gz] = x2_finish()
     z2_start()
-    relay2()
+    far_on2()
+    near2()
     far2()
+    q2_out = pltpu.make_async_copy(q2_ref, q2_hbm, out_sem.at[1])
+    q2_out.start()
     total2 = z2_finish()
     (step2_col,) = as_columns((norm2 / total2[0:1],))
-    near2()
-
-    outs = []
-    for i in range(CHIPS):
-        at = pl.ds(i * bs, bs)
-        b = b_ref[:, at]
-        r1 = b - step1_col * q1_ref[:, at]
-        d2 = r1 + ratio_col * b
-        sol_ref[:, at] = step1_col * b + step2_col * d2
-        res_ref[:, at] = r1 - step2_col * q2_ref[:, at]
-        outs.append(pltpu.make_async_copy(sol_ref.at[:, at], sol_hbm.at[:, at], out_sem.at[2 * i]))
-        outs.append(pltpu.make_async_copy(res_ref.at[:, at], res_hbm.at[:, at], out_sem.at[2 * i + 1]))
-        outs[-2].start()
-        outs[-1].start()
+    coef_ref[...] = jnp.where(lane == 0, step1_col, jnp.where(lane == 1, ratio_col, step2_col))
 
     for k in range(1, 8):
         flag_copy(k).wait_send()
@@ -554,17 +558,18 @@
     def _():
         halo_x(forward_dev, me).wait_send()
         halo_b(forward_dev, me).wait_send()
-        halo_q(forward_dev).wait_send()
         pass_on(x_ref, half_x, 0, h).wait_send()
         pass_on(bh_ref, half, 1, h).wait_send()
-        pass_on(qh_ref, half, 2, h).wait_send()
+        for c in range(chunks):
+            edge_q(forward_dev, c).wait_send()
+            edge_on(h, c).wait_send()
 
     @pl.when(y == CHIPS - 1)
     def _():
         group_copy.wait_send()
 
-    for o in outs:
-        o.wait()
+    q1_out.wait()
+    q2_out.wait()
 
 
 def body(features, inv_scale, signal, noise_var, right_side, block_pairs):
@@ -572,19 +577,18 @@
     bs = local // CHIPS
     own = bs // 2
     nx, nz = TORUS[lax.axis_size("blk")]
-    inv = jnp.broadcast_to((inv_scale * (W / 16.0))[:, None], (F, 128))
     vmem = pltpu.VMEM
     dma = pltpu.SemaphoreType.DMA
     f32, bf16 = jnp.float32, jnp.bfloat16
     hbm = pl.BlockSpec(memory_space=pl.ANY)
     smem = pl.BlockSpec(memory_space=pltpu.SMEM)
     shape = jax.ShapeDtypeStruct(right_side.shape, f32)
-    return pl.pallas_call(
+    q1, q2, coef = pl.pallas_call(
         functools.partial(kernel, nx, nz, bs),
         name="conjugate_gradients",
-        out_shape=(shape, shape),
+        out_shape=(shape, shape, jax.ShapeDtypeStruct((R, 128), f32)),
         in_specs=[hbm, pl.BlockSpec(memory_space=pltpu.VMEM), smem, hbm, hbm, smem],
-        out_specs=(hbm, hbm),
+        out_specs=(hbm, hbm, pl.BlockSpec(memory_space=pltpu.VMEM)),
         scratch_shapes=[
             vmem((F, 3 * bs), f32),
             vmem((3 * bs, TERMS), bf16),
@@ -606,23 +610,27 @@
             vmem((2, 8, 8, 128), f32),
             vmem((2, nx, 8, 128), f32),
             vmem((2, nz, 8, 128), f32),
-            vmem((R, local), f32),
-            vmem((R, local), f32),
+            vmem((1, own), f32),
             dma((6,)),
-            dma((8,)),
-            dma((6,)),
-            dma((6,)),
+            dma((2,)),
+            dma((4,)),
+            dma((4,)),
+            dma((2, own // LANES)),
+            dma((2, own // LANES)),
             dma((8,)),
             dma((8,)),
             dma((2, 3, 8)),
             dma((2, 3, 8)),
-            dma((2, 7)),
-            dma((2, 8)),
+            dma((2, 7, own // LANES)),
+            dma((2, 8, own // LANES)),
         ],
         compiler_params=pltpu.CompilerParams(
             collective_id=0, has_side_effects=True, vmem_limit_bytes=60 * 1024 * 1024
         ),
-    )(features, inv, signal, noise_var.reshape(1, -1), right_side, block_pairs)
+    )(features, inv_scale.reshape(1, -1), signal, noise_var.reshape(1, -1), right_side, block_pairs)
+    step1, ratio, step2 = coef[:, 0:1], coef[:, 1:2], coef[:, 2:3]
+    residual = right_side - step1 * q1
+    return step1 * right_side + step2 * (residual + ratio * right_side), residual - step2 * q2
 
 
 def solution(mesh):

time: 70.2 us -> 69.9 us (level)
  local copies, waits for them, and re-layouts: 4.02 us -> 1.05 us
  other arithmetic: 0.66 us -> 3.24 us
    unnamed x4 -> x2, local copies, waits for them, and re-layouts: 3.32 us -> 0.01 us
    sub x0 -> x1, other arithmetic: none -> 3.24 us  [body(): residual - step2 * q2]
    slice x0 -> x1, local copies, waits for them, and re-layouts: none -> 1.05 us  [body(): step1, ratio, step2 = (coef[:, 0:1], coef[:, 1:2], coef[:, 2:3])]
where the time goes in v2:
time: 69.9 us; the launch traced here: 69.7 us
  Pallas kernels  64 us (92%)
  other arithmetic  3.24 us (5%)
  between operations  1.39 us (2%)
  local copies, waits for them, and re-layouts  1.05 us (2%)
    pallas_call x1, Pallas kernels, body(): pl.pallas_call(functools.partial(kernel, nx, nz, bs), name='conjugate_gra...  64 us
    sub x1, other arithmetic, body(): residual - step2 * q2  3.24 us

profile of v2, /device:TPU:1, one launch (start us, length us, event | category | flops | bytes accessed | tf_op | source)
XLA Modules:
  0.0 69.7 jit_solution(13128834849865221357)
XLA Ops:
  0.6 0.0 copy-start
  1.4 64.0 %conjugate_gradients.1 = (f32[32,8192]{1,0:T(8,128)}, f32[32,8192]{1,0:T(8,128)}, f32[32,128]{1,0:T(8,128)}) custom-call(f32[64,8192]{1,0:T(8,128)} %x_hbm.1, f32[1,64]{1,0:T(1,128)} %bitcast.3, f32[1]{0:T(128)S(6)} %copy.8.sig_ref, f32[1,8192]{1,0:T(1,128)} %bitcast.2, f32[32,8192]{1,0:T(8,128)} %b_hbm.1, s32[2,2]{1,0:T(2,128)} %pairs_ref.1), custom_call_target="tpu_custom_call" | custom-call | tf_op jit(solution)/shard_map/conjugate_gradients/pallas_call | solution.py:586
  65.4 1.0 %slice_reduce_fusion.2 = (f32[32]{0:T(128)S(1)}, f32[32]{0:T(128)S(1)}, f32[32]{0:T(128)S(1)}) fusion(f32[32,128]{1,0:T(8,128)} %get-tuple-element.5), kind=kLoop, calls=%fused_computation.5 | loop fusion | bytes 768 | tf_op jit(solution)/shard_map/slice | solution.py:631
  66.4 0.0 copy-done
  66.4 3.2 %multiply_subtract_fusion = (f32[32,8192]{1,0:T(8,128)}, f32[32,8192]{1,0:T(8,128)}) fusion(f32[32,8192]{1,0:T(8,128)} %get-tuple-element.7, f32[32,8192]{1,0:T(8,128)S(1)} %copy-done, f32[32,8192]{1,0:T(8,128)} %get-tuple-element.6, f32[32]{0:T(128)S(1)} %get-tuple-element.10, f32[32]{0:T(128)S(1)} %get-tuple-element.8, f32[32]{0:T(128)S(1)} %get-tuple-element.9), kind=kLoop, calls=%fused_computation | loop fusion | flops 2359296 | bytes 5243264 | tf_op jit(solution)/shard_map/sub | solution.py:633
Async XLA Ops:
  0.6 65.8 %copy-start = (f32[32,8192]{1,0:T(8,128)S(1)}, f32[32,8192]{1,0:T(8,128)}, u32[]{:S(2)}) copy-start(f32[32,8192]{1,0:T(8,128)} %b_hbm.1) | copy-start | bytes 3145732

commit v3 on v2

--- a/solution.py
+++ b/solution.py
@@ -68,7 +68,7 @@
     return ((c2 * u + c1) * u + c0) * jnp.exp2(u) * (u2 * u2)
 
 
-def tile_pass(slot, ch, bs, l_ref, r_ref, k_ref, v_ref, p_ref, s_ref, sig, sq_ref, h_ref, after=None):
+def tile_pass(slot, ch, bs, l_ref, r_ref, k_ref, v_ref, p_ref, s_ref, sig, sq_ref, h_ref, multiply=True):
     c0, c1, c2 = sig * Q0, sig * Q1, sig * Q2
     n = bs // ch
     base = slot * bs
@@ -85,12 +85,17 @@
         def values(i, buf, sums):
             t = tile_values(sq_ref[buf], c0, c1, c2)
             half = t.astype(jnp.bfloat16)
-            h_ref[buf] = half
             k_ref[at(i), cols] = half
+            if multiply:
+                h_ref[buf] = half
+            if slot == 0:
+                return sums
             return sums + jnp.sum(t.reshape(ch // 8, 8, LANES), axis=0)
 
         def prod(i, buf, acc):
-            return acc + jnp.dot(v_ref[:, at(i)], h_ref[buf], preferred_element_type=jnp.float32)
+            if not multiply:
+                return acc
+            return acc + jnp.dot(v_ref[0:R, at(i)], h_ref[buf], preferred_element_type=jnp.float32)
 
         acc = jnp.zeros((R, LANES), jnp.float32)
         sums = jnp.zeros((8, LANES), jnp.float32)
@@ -113,10 +118,9 @@
         sums = values(n - 1, 1, sums)
         acc = prod(n - 2, 0, acc)
         acc = prod(n - 1, 1, acc)
-        p_ref[slot, :, cols] = acc
+        if multiply:
+            p_ref[slot, :, cols] = acc
         s_ref[slot, :, cols] = jnp.broadcast_to(jnp.sum(sums, axis=0, keepdims=True), (8, LANES))
-        if after is not None:
-            after(j, cols)
         return 0
 
     lax.fori_loop(0, p_ref.shape[2] // LANES, lanes, 0)
@@ -222,10 +226,8 @@
         at = pl.ds(pl.multiple_of(h * own + i * ch, ch), ch)
         r_ref[:, i * ch : (i + 1) * ch] = right_terms(x_ref[:, at], inv)
     load_b.wait()
-    v_ref[:, 0:bs] = b_ref[:, block(y)].astype(jnp.bfloat16)
-    v_ref[:, bs : 2 * bs] = b_ref[:, block(first)].astype(jnp.bfloat16)
-    load_x1.wait()
-    prepare(1)
+    v_ref[0:R, 0:bs] = b_ref[:, block(y)].astype(jnp.bfloat16)
+    v_ref[0:R, bs : 2 * bs] = b_ref[:, block(first)].astype(jnp.bfloat16)
 
     pl.semaphore_wait(barrier, 5 + nx + nz + jnp.where(edge, 1, 0))
 
@@ -234,14 +236,14 @@
     other = pl.ds(pl.multiple_of((1 - h) * own, own), own)
     other_x = pl.ds(pl.multiple_of(2 * bs + (1 - h) * own, own), own)
 
-    def halo_x(device, src):
-        return pltpu.make_async_remote_copy(
-            x_hbm.at[:, piece(src)], x_ref.at[:, half_x], halo_send.at[0], halo_recv.at[h],
+    def halo_x(device):
+        return pltpu.make_async_remote_copy(
+            x_ref.at[:, half], x_ref.at[:, half_x], halo_send.at[0], halo_recv.at[h],
             device_id=device, device_id_type=MESH)
 
-    def halo_b(device, src):
-        return pltpu.make_async_remote_copy(
-            b_hbm.at[:, piece(src)], bh_ref.at[:, half], halo_send.at[1], halo_recv.at[2 + h],
+    def halo_b(device):
+        return pltpu.make_async_remote_copy(
+            b_ref.at[:, mine], bh_ref.at[:, half], halo_send.at[1], halo_recv.at[2 + h],
             device_id=device, device_id_type=MESH)
 
     chunks = own // LANES
@@ -269,13 +271,13 @@
 
     @pl.when(y == CHIPS - 1)
     def _():
-        halo_x(forward_dev, me).start()
-        halo_b(forward_dev, me).start()
+        halo_x(forward_dev).start()
+        halo_b(forward_dev).start()
 
     @pl.when(y == 0)
     def _():
-        halo_x(backward_dev, me).start()
-        halo_b(backward_dev, me).start()
+        halo_x(backward_dev).start()
+        halo_b(backward_dev).start()
 
     def flag_copy(k):
         return pltpu.make_async_remote_copy(
@@ -290,6 +292,8 @@
 
     for k in range(1, 8):
         flag_copy(k).start()
+    load_x1.wait()
+    prepare(1)
 
     sig = sig_ref[0]
     passes = functools.partial(
@@ -317,19 +321,27 @@
     @pl.when(jnp.logical_not(edge))
     def _():
         load_x2.wait()
-        load_bh.wait()
 
     @pl.when(edge)
     def _():
         pass_on(x_ref, half_x, 0, h).wait_recv()
         pass_on(x_ref, half_x, 0, h).start()
+        pass_on(x_ref, other_x, 0, 1 - h).wait_recv()
+
+    prepare(2)
+    passes(2, ch, bs, multiply=False)
+
+    @pl.when(jnp.logical_not(edge))
+    def _():
+        load_bh.wait()
+
+    @pl.when(edge)
+    def _():
         pass_on(bh_ref, half, 1, h).wait_recv()
         pass_on(bh_ref, half, 1, h).start()
-        pass_on(x_ref, other_x, 0, 1 - h).wait_recv()
         pass_on(bh_ref, other, 1, 1 - h).wait_recv()
 
-    prepare(2)
-    v_ref[:, 2 * bs : 3 * bs] = bh_ref[...].astype(jnp.bfloat16)
+    v_ref[0:R, 2 * bs : 3 * bs] = bh_ref[...].astype(jnp.bfloat16)
     load_noise.wait()
 
     @pl.when(y == 0)
@@ -359,8 +371,11 @@
     def image(cols, vec):
         return diag_ref[:, cols] * vec + (p_ref[0, :, cols] + flag_first * p_ref[1, :, cols] + flag_last * p_ref[2, :, cols])
 
-    def first_image(j, cols):
+    def first_image(j, _):
+        cols = pl.ds(pl.multiple_of(j * LANES, LANES), LANES)
         at = slab(me, j)
+        rows = pl.ds(2 * bs, bs)
+        p_ref[2, :, cols] = jnp.dot(v_ref[0:R, rows], k_ref[rows, cols], preferred_element_type=jnp.float32)
         diag_ref[:, cols] = noise_ref[:, cols] + flag_first * s_ref[1, 0:1, cols] + flag_last * s_ref[2, 0:1, cols]
         q1_ref[:, at] = image(cols, b_ref[:, at])
         hand_out(0, q1_ref, j)
@@ -373,7 +388,9 @@
         def _():
             edge_q(backward_dev, j).start()
 
-    passes(2, ch, bs, after=first_image)
+        return 0
+
+    lax.fori_loop(0, chunks, first_image, 0)
 
     lane = lax.broadcasted_iota(jnp.int32, (R, 128), 1)
 
@@ -421,6 +438,11 @@
             sum_copies(t, sz_ref, 2, nz, gz, lambda p: (gx * nz + p, me)),
         )
 
+    def own_chip(t):
+        for c in range(chunks):
+            ref = (q1_ref, q2_ref)[t]
+            part_copy(t, ref, y * 2 + 1 - h, c, 0, partner).wait_recv()
+
     def parts(t, ref):
         def arrived(which, c):
             part_copy(t, ref, which, c, 0, partner).wait_recv()
@@ -444,7 +466,6 @@
 
         def near():
             for c in range(chunks):
-                arrived(y * 2 + 1 - h, c)
                 arrived(down * 2 + 1 - h, c)
                 arrived(up * 2 + 1 - h, c)
 
@@ -464,14 +485,30 @@
 
         return relay, near, far_on, far, drain
 
-    b_own = b_ref[:, mine]
-    q_own = q1_ref[:, mine]
-    set_stats(0, (b_own * b_own, b_own * q_own, q_own * q_own))
+    relay, near, far_on, far, drain = parts(0, q1_ref)
+    relay2, near2, far_on2, far2, drain2 = parts(1, q2_ref)
     (a_start, a_finish, a_drain), (x_start, x_finish, x_drain), (z_start, z_finish, z_drain) = stages(0)
-    relay, near, far_on, far, drain = parts(0, q1_ref)
-    a_start()
-    sx_ref[0, gx] = a_finish()
-    x_start()
+
+    def two_terms(slot, q):
+        at = pl.ds(slot * bs, bs)
+        hi = q.astype(jnp.bfloat16)
+        v_ref[0:R, at] = hi
+        v_ref[R : 2 * R, at] = (q - hi.astype(jnp.float32)).astype(jnp.bfloat16)
+
+    def product(slot, cols):
+        rows = pl.ds(slot * bs, bs)
+        both = jnp.dot(v_ref[:, rows], k_ref[rows, cols], preferred_element_type=jnp.float32)
+        return both[0:R] + both[R : 2 * R]
+
+    own_chip(0)
+    two_terms(0, q1_ref[:, block(y)])
+
+    def own_lanes(j, _):
+        cols = pl.ds(pl.multiple_of(j * LANES, LANES), LANES)
+        p_ref[0, :, cols] = product(0, cols)
+        return 0
+
+    lax.fori_loop(0, chunks, own_lanes, 0)
     relay()
 
     @pl.when(edge)
@@ -480,84 +517,70 @@
             edge_on(h, c).wait_recv()
             edge_on(h, c).start()
 
+    near()
+
+    @pl.when(edge)
+    def _():
+        for c in range(chunks):
+            edge_on(1 - h, c).wait_recv()
+
+    @pl.when(jnp.logical_not(edge))
+    def _():
+        qh_ref[...] = q1_ref[:, block(last)]
+
+    two_terms(1, q1_ref[:, block(first)])
+    two_terms(2, qh_ref[...])
+
+    def second_image(j, _):
+        cols = pl.ds(pl.multiple_of(j * LANES, LANES), LANES)
+        p_ref[1, :, cols] = product(1, cols)
+        p_ref[2, :, cols] = product(2, cols)
+        at = slab(me, j)
+        q2_ref[:, at] = image(cols, q1_ref[:, at])
+        hand_out(1, q2_ref, j)
+        return 0
+
+    lax.fori_loop(0, chunks, second_image, 0)
+    b_own, q_own, w_own = b_ref[:, mine], q1_ref[:, mine], q2_ref[:, mine]
+    set_stats(0, (b_own * b_own, b_own * q_own, q_own * q_own, b_own * w_own, q_own * w_own))
+    a_start()
+    far_on()
+    sx_ref[0, gx] = a_finish()
+    x_start()
+    relay2()
     sz_ref[0, gz] = x_finish()
     z_start()
-    far_on()
-
-    total = z_finish()
-    norm, curve, square = total[0:1], total[1:2], total[2:3]
-    step1 = norm / curve
-    norm2 = norm - 2.0 * step1 * curve + step1 * step1 * square
-    ratio = norm2 / norm
-
-    def as_columns(rows):
-        stacked = jnp.zeros((8, 128), jnp.float32)
-        for k, a in enumerate(rows):
-            stacked = jnp.where(row == k, a, stacked)
-        turned = jnp.concatenate([stacked, jnp.zeros((120, 128), jnp.float32)], 0).T
-        return [turned[0:R, k : k + 1] for k in range(len(rows))]
-
-    step1_col, ratio_col = as_columns((step1, ratio))
-    near()
-
-    @pl.when(edge)
-    def _():
-        for c in range(chunks):
-            edge_on(1 - h, c).wait_recv()
-
-    @pl.when(jnp.logical_not(edge))
-    def _():
-        qh_ref[...] = q1_ref[:, block(last)]
-
-    def next_direction(b, q):
-        return (b - step1_col * q) + ratio_col * b
-
-    v_ref[:, 0:bs] = next_direction(b_ref[:, block(y)], q1_ref[:, block(y)]).astype(jnp.bfloat16)
-    v_ref[:, bs : 2 * bs] = next_direction(b_ref[:, block(first)], q1_ref[:, block(first)]).astype(jnp.bfloat16)
-    v_ref[:, 2 * bs : 3 * bs] = next_direction(bh_ref[...], qh_ref[...]).astype(jnp.bfloat16)
-
-    def lanes(j, _):
-        cols = pl.ds(pl.multiple_of(j * LANES, LANES), LANES)
-        for slot in range(3):
-            rows = pl.ds(slot * bs, bs)
-            p_ref[slot, :, cols] = jnp.dot(v_ref[:, rows], k_ref[rows, cols], preferred_element_type=jnp.float32)
-        at = slab(me, j)
-        q2_ref[:, at] = image(cols, next_direction(b_ref[:, at], q1_ref[:, at]))
-        hand_out(1, q2_ref, j)
-        return 0
-
-    lax.fori_loop(0, chunks, lanes, 0)
-    d_own = next_direction(b_own, q1_ref[:, mine])
-    set_stats(1, (d_own * q2_ref[:, mine],))
-    (a2_start, a2_finish, a2_drain), (x2_start, x2_finish, x2_drain), (z2_start, z2_finish, z2_drain) = stages(1)
-    relay2, near2, far_on2, far2, drain2 = parts(1, q2_ref)
-    a2_start()
     far()
     q1_out = pltpu.make_async_copy(q1_ref, q1_hbm, out_sem.at[0])
     q1_out.start()
-    sx_ref[1, gx] = a2_finish()
-    x2_start()
-    relay2()
-    sz_ref[1, gz] = x2_finish()
-    z2_start()
     far_on2()
+    own_chip(1)
     near2()
     far2()
     q2_out = pltpu.make_async_copy(q2_ref, q2_hbm, out_sem.at[1])
     q2_out.start()
-    total2 = z2_finish()
-    (step2_col,) = as_columns((norm2 / total2[0:1],))
-    coef_ref[...] = jnp.where(lane == 0, step1_col, jnp.where(lane == 1, ratio_col, step2_col))
+    total = z_finish()
+    norm, curve, square, cross, cube = [total[k : k + 1] for k in range(5)]
+    step1 = norm / curve
+    norm2 = norm - 2.0 * step1 * curve + step1 * step1 * square
+    ratio = norm2 / norm
+    grown = 1.0 + ratio
+    curve2 = grown * (grown * curve - step1 * (square + cross)) + step1 * step1 * cube
+    step2 = norm2 / curve2
+    stacked = jnp.zeros((8, 128), jnp.float32)
+    for k, a in enumerate((step1, ratio, step2)):
+        stacked = jnp.where(row == k, a, stacked)
+    coef_ref[...] = jnp.concatenate([stacked, jnp.zeros((120, 128), jnp.float32)], 0).T[0:R]
 
     for k in range(1, 8):
         flag_copy(k).wait_send()
-    for wait in (a_drain, x_drain, z_drain, drain, a2_drain, x2_drain, z2_drain, drain2):
+    for wait in (a_drain, x_drain, z_drain, drain, drain2):
         wait()
 
     @pl.when(edge)
     def _():
-        halo_x(forward_dev, me).wait_send()
-        halo_b(forward_dev, me).wait_send()
+        halo_x(forward_dev).wait_send()
+        halo_b(forward_dev).wait_send()
         pass_on(x_ref, half_x, 0, h).wait_send()
         pass_on(bh_ref, half, 1, h).wait_send()
         for c in range(chunks):
@@ -599,7 +622,7 @@
             vmem((R, local), f32),
             vmem((R, bs), f32),
             vmem((R, local), f32),
-            vmem((R, 3 * bs), bf16),
+            vmem((2 * R, 3 * bs), bf16),
             vmem((3, R, own), f32),
             vmem((3, 8, own), f32),
             vmem((1, own), f32),
@@ -607,9 +630,9 @@
             vmem((2, bs // 4, LANES), bf16),
             vmem((8, 8, 128), f32),
             vmem((3, 8, 128), f32),
-            vmem((2, 8, 8, 128), f32),
-            vmem((2, nx, 8, 128), f32),
-            vmem((2, nz, 8, 128), f32),
+            vmem((1, 8, 8, 128), f32),
+            vmem((1, nx, 8, 128), f32),
+            vmem((1, nz, 8, 128), f32),
             vmem((1, own), f32),
             dma((6,)),
             dma((2,)),
@@ -619,8 +642,8 @@
             dma((2, own // LANES)),
             dma((8,)),
             dma((8,)),
-            dma((2, 3, 8)),
-            dma((2, 3, 8)),
+            dma((1, 3, 8)),
+            dma((1, 3, 8)),
             dma((2, 7, own // LANES)),
             dma((2, 8, own // LANES)),
         ],
@@ -630,7 +653,8 @@
     )(features, inv_scale.reshape(1, -1), signal, noise_var.reshape(1, -1), right_side, block_pairs)
     step1, ratio, step2 = coef[:, 0:1], coef[:, 1:2], coef[:, 2:3]
     residual = right_side - step1 * q1
-    return step1 * right_side + step2 * (residual + ratio * right_side), residual - step2 * q2
+    image = (1.0 + ratio) * q1 - step1 * q2
+    return step1 * right_side + step2 * (residual + ratio * right_side), residual - step2 * image
 
 
 def solution(mesh):

time: 69.9 us -> 65 us (0.930)
  Pallas kernels: 64 us -> 59 us
  other arithmetic: 3.24 us -> 4.39 us
  local copies, waits for them, and re-layouts: 1.05 us -> 0.01 us
    pallas_call x1, Pallas kernels: 64 us -> 59 us  [body(): pl.pallas_call(functools.partial(kernel, nx, nz, bs), name='conjugate_gra...]
    add x0 -> x1, other arithmetic: none -> 1.05 us  [body(): image = (1.0 + ratio) * q1 - step1 * q2]
    slice x1 -> x0, local copies, waits for them, and re-layouts: 1.05 us -> none  [body(): step1, ratio, step2 = (coef[:, 0:1], coef[:, 1:2], coef[:, 2:3])]
where the time goes in v3:
time: 65 us; the launch traced here: 64.8 us
  Pallas kernels  59 us (91%)
  other arithmetic  4.39 us (7%)
  between operations  1.39 us (2%)
    pallas_call x1, Pallas kernels, body(): pl.pallas_call(functools.partial(kernel, nx, nz, bs), name='conjugate_gra...  59 us
    sub x1, other arithmetic, body(): residual - step2 * image  3.34 us

profile of v3, /device:TPU:1, one launch (start us, length us, event | category | flops | bytes accessed | tf_op | source)
XLA Modules:
  0.0 64.8 jit_solution(17242952557978899189)
XLA Ops:
  0.6 0.0 copy-start
  1.4 59.0 %conjugate_gradients.1 = (f32[32,8192]{1,0:T(8,128)}, f32[32,8192]{1,0:T(8,128)}, f32[32,128]{1,0:T(8,128)}) custom-call(f32[64,8192]{1,0:T(8,128)} %x_hbm.1, f32[1,64]{1,0:T(1,128)} %bitcast.3, f32[1]{0:T(128)S(6)} %copy.8.sig_ref, f32[1,8192]{1,0:T(1,128)} %bitcast.2, f32[32,8192]{1,0:T(8,128)} %b_hbm.1, s32[2,2]{1,0:T(2,128)} %pairs_ref.1), custom_call_target="tpu_custom_call" | custom-call | tf_op jit(solution)/shard_map/conjugate_gradients/pallas_call | solution.py:609
  60.4 1.0 %add_reduce_fusion = (f32[32]{0:T(128)S(1)}, f32[32]{0:T(128)S(1)}, f32[32]{0:T(128)S(1)}, f32[32]{0:T(128)S(1)}) fusion(f32[32,128]{1,0:T(8,128)} %get-tuple-element.5), kind=kLoop, calls=%fused_computation.3 | loop fusion | flops 32 | bytes 896 | tf_op jit(solution)/shard_map/add | solution.py:656
  61.5 0.0 copy-done
  61.5 3.3 %multiply_subtract_fusion = (f32[32,8192]{1,0:T(8,128)}, f32[32,8192]{1,0:T(8,128)}) fusion(f32[32,8192]{1,0:T(8,128)} %get-tuple-element.7, f32[32,8192]{1,0:T(8,128)} %get-tuple-element.6, f32[32,8192]{1,0:T(8,128)S(1)} %copy-done, f32[32]{0:T(128)S(1)} %get-tuple-element.8, f32[32]{0:T(128)S(1)} %get-tuple-element.10, f32[32]{0:T(128)S(1)} %get-tuple-element.11, ...), kind=kLoop, calls=%fused_computation | loop fusion | flops 3145728 | bytes 5243392 | tf_op jit(solution)/shard_map/sub | solution.py:657
Async XLA Ops:
  0.6 60.8 %copy-start = (f32[32,8192]{1,0:T(8,128)S(1)}, f32[32,8192]{1,0:T(8,128)}, u32[]{:S(2)}) copy-start(f32[32,8192]{1,0:T(8,128)} %b_hbm.1) | copy-start | bytes 3145732

commit v4 on v3

--- a/solution.py
+++ b/solution.py
@@ -68,7 +68,7 @@
     return ((c2 * u + c1) * u + c0) * jnp.exp2(u) * (u2 * u2)
 
 
-def tile_pass(slot, ch, bs, l_ref, r_ref, k_ref, v_ref, p_ref, s_ref, sig, sq_ref, h_ref, multiply=True):
+def tile_pass(slot, ch, bs, l_ref, r_ref, k_ref, v_ref, p_ref, s_ref, sig, sq_ref, h_ref, after=None):
     c0, c1, c2 = sig * Q0, sig * Q1, sig * Q2
     n = bs // ch
     base = slot * bs
@@ -86,15 +86,12 @@
             t = tile_values(sq_ref[buf], c0, c1, c2)
             half = t.astype(jnp.bfloat16)
             k_ref[at(i), cols] = half
-            if multiply:
-                h_ref[buf] = half
+            h_ref[buf] = half
             if slot == 0:
                 return sums
             return sums + jnp.sum(t.reshape(ch // 8, 8, LANES), axis=0)
 
         def prod(i, buf, acc):
-            if not multiply:
-                return acc
             return acc + jnp.dot(v_ref[0:R, at(i)], h_ref[buf], preferred_element_type=jnp.float32)
 
         acc = jnp.zeros((R, LANES), jnp.float32)
@@ -118,9 +115,10 @@
         sums = values(n - 1, 1, sums)
         acc = prod(n - 2, 0, acc)
         acc = prod(n - 1, 1, acc)
-        if multiply:
-            p_ref[slot, :, cols] = acc
+        p_ref[slot, :, cols] = acc
         s_ref[slot, :, cols] = jnp.broadcast_to(jnp.sum(sums, axis=0, keepdims=True), (8, LANES))
+        if after is not None:
+            after(j, cols)
         return 0
 
     lax.fori_loop(0, p_ref.shape[2] // LANES, lanes, 0)
@@ -169,13 +167,16 @@
     for k in range(1, nz):
         greet((gx * nz + (gz + k) % nz, me))
 
-    @pl.when(y == CHIPS - 1)
-    def _():
-        greet((after, h))
-
-    @pl.when(y == 0)
-    def _():
-        greet((before, (CHIPS - 1) * 2 + h))
+    top = y == CHIPS - 1
+    crossing = (jnp.where(top, after, before), jnp.where(top, h, (CHIPS - 1) * 2 + h))
+    beside = (jnp.where(top, before, after), me)
+    beside_block = jnp.where(top, 0, CHIPS - 1)
+
+    @pl.when(edge)
+    def _():
+        greet(crossing)
+        greet((after, me))
+        greet((before, me))
 
     load_x0 = pltpu.make_async_copy(x_hbm.at[:, block(y)], x_ref.at[:, pl.ds(0, bs)], local_sem.at[0])
     load_x1 = pltpu.make_async_copy(x_hbm.at[:, block(first)], x_ref.at[:, pl.ds(bs, bs)], local_sem.at[1])
@@ -229,22 +230,36 @@
     v_ref[0:R, 0:bs] = b_ref[:, block(y)].astype(jnp.bfloat16)
     v_ref[0:R, bs : 2 * bs] = b_ref[:, block(first)].astype(jnp.bfloat16)
 
-    pl.semaphore_wait(barrier, 5 + nx + nz + jnp.where(edge, 1, 0))
-
-    half = pl.ds(pl.multiple_of(h * own, own), own)
-    half_x = pl.ds(pl.multiple_of(2 * bs + h * own, own), own)
-    other = pl.ds(pl.multiple_of((1 - h) * own, own), own)
-    other_x = pl.ds(pl.multiple_of(2 * bs + (1 - h) * own, own), own)
-
-    def halo_x(device):
+    pl.semaphore_wait(barrier, 5 + nx + nz + jnp.where(edge, 3, 0))
+
+    sub = own // 2
+
+    def halo_at(base, side, k):
+        return pl.ds(pl.multiple_of(base + side * own + k * sub, sub), sub)
+
+    def halo(kind, k):
+        ref, base = ((x_ref, 2 * bs), (bh_ref, 0))[kind]
+        if kind == 0:
+            src = x_ref.at[:, halo_at(0, h, 0)] if k == 0 else x_hbm.at[:, halo_at(beside_block * bs, h, 1)]
+        else:
+            src = b_ref.at[:, halo_at((y if k == 0 else beside_block) * bs, h, k)]
         return pltpu.make_async_remote_copy(
-            x_ref.at[:, half], x_ref.at[:, half_x], halo_send.at[0], halo_recv.at[h],
-            device_id=device, device_id_type=MESH)
-
-    def halo_b(device):
+            src, ref.at[:, halo_at(base, h, k)], halo_send.at[2 * kind + k], halo_recv.at[kind, h, k],
+            device_id=crossing if k == 0 else beside, device_id_type=MESH)
+
+    def pass_on(kind, side, k):
+        ref, base = ((x_ref, 2 * bs), (bh_ref, 0))[kind]
+        at = halo_at(base, side, k)
         return pltpu.make_async_remote_copy(
-            b_ref.at[:, mine], bh_ref.at[:, half], halo_send.at[1], halo_recv.at[2 + h],
-            device_id=device, device_id_type=MESH)
+            ref.at[:, at], ref.at[:, at], halo_send.at[4 + 2 * kind + k], halo_recv.at[kind, side, k],
+            device_id=partner, device_id_type=MESH)
+
+    def take_halo(kind):
+        for k in range(2):
+            pass_on(kind, h, k).wait_recv()
+            pass_on(kind, h, k).start()
+        for k in range(2):
+            pass_on(kind, 1 - h, k).wait_recv()
 
     chunks = own // LANES
 
@@ -261,23 +276,11 @@
             qh_ref.at[:, slab(side, c)], qh_ref.at[:, slab(side, c)], edge_send.at[1, c], edge_recv.at[side, c],
             device_id=partner, device_id_type=MESH)
 
-    def pass_on(ref, at, k, sem):
-        return pltpu.make_async_remote_copy(
-            ref.at[:, at], ref.at[:, at], halo_send.at[2 + k], halo_recv.at[2 * k + sem],
-            device_id=partner, device_id_type=MESH)
-
-    forward_dev = (after, h)
-    backward_dev = (before, (CHIPS - 1) * 2 + h)
-
-    @pl.when(y == CHIPS - 1)
-    def _():
-        halo_x(forward_dev).start()
-        halo_b(forward_dev).start()
-
-    @pl.when(y == 0)
-    def _():
-        halo_x(backward_dev).start()
-        halo_b(backward_dev).start()
+    @pl.when(edge)
+    def _():
+        for kind in range(2):
+            for k in range(2):
+                halo(kind, k).start()
 
     def flag_copy(k):
         return pltpu.make_async_remote_copy(
@@ -310,7 +313,7 @@
     group_ref[0] = total_flags
     group_copy = pltpu.make_async_remote_copy(
         group_ref.at[0], group_ref.at[1], flag_send.at[0], flag_recv.at[0],
-        device_id=forward_dev, device_id_type=MESH)
+        device_id=crossing, device_id_type=MESH)
 
     @pl.when(y == CHIPS - 1)
     def _():
@@ -321,25 +324,17 @@
     @pl.when(jnp.logical_not(edge))
     def _():
         load_x2.wait()
+        load_bh.wait()
 
     @pl.when(edge)
     def _():
-        pass_on(x_ref, half_x, 0, h).wait_recv()
-        pass_on(x_ref, half_x, 0, h).start()
-        pass_on(x_ref, other_x, 0, 1 - h).wait_recv()
+        take_halo(0)
 
     prepare(2)
-    passes(2, ch, bs, multiply=False)
-
-    @pl.when(jnp.logical_not(edge))
-    def _():
-        load_bh.wait()
 
     @pl.when(edge)
     def _():
-        pass_on(bh_ref, half, 1, h).wait_recv()
-        pass_on(bh_ref, half, 1, h).start()
-        pass_on(bh_ref, other, 1, 1 - h).wait_recv()
+        take_halo(1)
 
     v_ref[0:R, 2 * bs : 3 * bs] = bh_ref[...].astype(jnp.bfloat16)
     load_noise.wait()
@@ -371,26 +366,17 @@
     def image(cols, vec):
         return diag_ref[:, cols] * vec + (p_ref[0, :, cols] + flag_first * p_ref[1, :, cols] + flag_last * p_ref[2, :, cols])
 
-    def first_image(j, _):
-        cols = pl.ds(pl.multiple_of(j * LANES, LANES), LANES)
+    def first_image(j, cols):
         at = slab(me, j)
-        rows = pl.ds(2 * bs, bs)
-        p_ref[2, :, cols] = jnp.dot(v_ref[0:R, rows], k_ref[rows, cols], preferred_element_type=jnp.float32)
         diag_ref[:, cols] = noise_ref[:, cols] + flag_first * s_ref[1, 0:1, cols] + flag_last * s_ref[2, 0:1, cols]
         q1_ref[:, at] = image(cols, b_ref[:, at])
         hand_out(0, q1_ref, j)
 
-        @pl.when(y == CHIPS - 1)
+        @pl.when(edge)
         def _():
-            edge_q(forward_dev, j).start()
-
-        @pl.when(y == 0)
-        def _():
-            edge_q(backward_dev, j).start()
-
-        return 0
-
-    lax.fori_loop(0, chunks, first_image, 0)
+            edge_q(crossing, j).start()
+
+    passes(2, ch, bs, after=first_image)
 
     lane = lax.broadcasted_iota(jnp.int32, (R, 128), 1)
 
@@ -579,12 +565,12 @@
 
     @pl.when(edge)
     def _():
-        halo_x(forward_dev).wait_send()
-        halo_b(forward_dev).wait_send()
-        pass_on(x_ref, half_x, 0, h).wait_send()
-        pass_on(bh_ref, half, 1, h).wait_send()
+        for kind in range(2):
+            for k in range(2):
+                halo(kind, k).wait_send()
+                pass_on(kind, h, k).wait_send()
         for c in range(chunks):
-            edge_q(forward_dev, c).wait_send()
+            edge_q(crossing, c).wait_send()
             edge_on(h, c).wait_send()
 
     @pl.when(y == CHIPS - 1)
@@ -593,6 +579,14 @@
 
     q1_out.wait()
     q2_out.wait()
+
+
+def combine(coef_ref, b_ref, q1_ref, q2_ref, sol_ref, res_ref):
+    step1, ratio, step2 = coef_ref[:, 0:1], coef_ref[:, 1:2], coef_ref[:, 2:3]
+    b, q1 = b_ref[...], q1_ref[...]
+    residual = b - step1 * q1
+    sol_ref[...] = step1 * b + step2 * (residual + ratio * b)
+    res_ref[...] = residual - step2 * ((1.0 + ratio) * q1 - step1 * q2_ref[...])
 
 
 def body(features, inv_scale, signal, noise_var, right_side, block_pairs):
@@ -636,8 +630,8 @@
             vmem((1, own), f32),
             dma((6,)),
             dma((2,)),
-            dma((4,)),
-            dma((4,)),
+            dma((8,)),
+            dma((2, 2, 2)),
             dma((2, own // LANES)),
             dma((2, own // LANES)),
             dma((8,)),
@@ -651,10 +645,15 @@
             collective_id=0, has_side_effects=True, vmem_limit_bytes=60 * 1024 * 1024
         ),
     )(features, inv_scale.reshape(1, -1), signal, noise_var.reshape(1, -1), right_side, block_pairs)
-    step1, ratio, step2 = coef[:, 0:1], coef[:, 1:2], coef[:, 2:3]
-    residual = right_side - step1 * q1
-    image = (1.0 + ratio) * q1 - step1 * q2
-    return step1 * right_side + step2 * (residual + ratio * right_side), residual - step2 * image
+    blocks = pl.BlockSpec((R, bs), lambda i: (0, i))
+    return pl.pallas_call(
+        combine,
+        name="combine",
+        grid=(CHIPS,),
+        out_shape=(shape, shape),
+        in_specs=[pl.BlockSpec((R, 128), lambda i: (0, 0)), blocks, blocks, blocks],
+        out_specs=(blocks, blocks),
+    )(coef, right_side, q1, q2)
 
 
 def solution(mesh):

time: 65 us -> 60.3 us (0.928)
  other arithmetic: 4.39 us -> 0 us
    pallas_call x1, Pallas kernels: 59 us -> 54.5 us  [body(): pl.pallas_call(functools.partial(kernel, nx, nz, bs), name='conjugate_gra...]
    pallas_call x0 -> x1, Pallas kernels: none -> 4.33 us  [body(): pl.pallas_call(combine, name='combine', grid=(CHIPS,), out_shape=(shape,...]
    sub x1 -> x0, other arithmetic: 3.34 us -> none  [body(): residual - step2 * image]
    add x1 -> x0, other arithmetic: 1.05 us -> none  [body(): image = (1.0 + ratio) * q1 - step1 * q2]
where the time goes in v4:
time: 60.3 us; the launch traced here: 60.1 us
  Pallas kernels  58.8 us (98%)
  between operations  1.28 us (2%)
    pallas_call x1, Pallas kernels, body(): pl.pallas_call(functools.partial(kernel, nx, nz, bs), name='conjugate_gra...  54.5 us
    pallas_call x1, Pallas kernels, body(): pl.pallas_call(combine, name='combine', grid=(CHIPS,), out_shape=(shape,...  4.33 us

profile of v4, /device:TPU:1, one launch (start us, length us, event | category | flops | bytes accessed | tf_op | source)
XLA Modules:
  0.0 60.1 jit_solution(570739868720943945)
XLA Ops:
  1.3 54.5 %conjugate_gradients.1 = (f32[32,8192]{1,0:T(8,128)}, f32[32,8192]{1,0:T(8,128)}, f32[32,128]{1,0:T(8,128)}) custom-call(f32[64,8192]{1,0:T(8,128)} %x_hbm.1, f32[1,64]{1,0:T(1,128)} %bitcast.3, f32[1]{0:T(128)S(6)} %copy.8.sig_ref, f32[1,8192]{1,0:T(1,128)} %bitcast.2, f32[32,8192]{1,0:T(8,128)} %b_ref.1, s32[2,2]{1,0:T(2,128)} %pairs_ref.1), custom_call_target="tpu_custom_call" | custom-call | tf_op jit(solution)/shard_map/conjugate_gradients/pallas_call | solution.py:603
  55.8 4.3 %combine.1 = (f32[32,8192]{1,0:T(8,128)}, f32[32,8192]{1,0:T(8,128)}) custom-call(f32[32,128]{1,0:T(8,128)} %get-tuple-element.5.coef_ref, f32[32,8192]{1,0:T(8,128)} %b_ref.1, f32[32,8192]{1,0:T(8,128)} %get-tuple-element.6.q1_ref, f32[32,8192]{1,0:T(8,128)} %get-tuple-element.7.q2_ref), custom_call_target="tpu_custom_call" | custom-call | tf_op jit(solution)/shard_map/combine/pallas_call | solution.py:649

commit v5 on v4

--- a/solution.py
+++ b/solution.py
@@ -127,11 +127,11 @@
 def kernel(
     nx, nz, bs,
     x_hbm, inv_ref, sig_ref, noise_hbm, b_hbm, pairs_ref,
-    q1_hbm, q2_hbm, coef_ref,
+    q1_out, q2_out, coef_ref,
     x_ref, l_ref, r_ref, k_ref, b_ref, bh_ref, q1_ref, qh_ref, q2_ref, v_ref,
     p_ref, s_ref, noise_ref, sq_ref, h_ref, flag_ref, group_ref, st_ref, sx_ref, sz_ref,
     diag_ref,
-    local_sem, out_sem, halo_send, halo_recv, edge_send, edge_recv, flag_send, flag_recv, sum_send, sum_recv, part_send, part_recv,
+    local_sem, halo_send, halo_recv, edge_send, edge_recv, flag_send, flag_recv, sum_send, sum_recv, part_send, part_recv,
 ):
     own = bs // 2
     ch = bs // 4
@@ -537,14 +537,12 @@
     sz_ref[0, gz] = x_finish()
     z_start()
     far()
-    q1_out = pltpu.make_async_copy(q1_ref, q1_hbm, out_sem.at[0])
-    q1_out.start()
+    q1_out[...] = q1_ref[...]
     far_on2()
     own_chip(1)
     near2()
     far2()
-    q2_out = pltpu.make_async_copy(q2_ref, q2_hbm, out_sem.at[1])
-    q2_out.start()
+    q2_out[...] = q2_ref[...]
     total = z_finish()
     norm, curve, square, cross, cube = [total[k : k + 1] for k in range(5)]
     step1 = norm / curve
@@ -577,16 +575,22 @@
     def _():
         group_copy.wait_send()
 
-    q1_out.wait()
-    q2_out.wait()
-
-
-def combine(coef_ref, b_ref, q1_ref, q2_ref, sol_ref, res_ref):
+
+def combine(bs, coef_ref, b_ref, q1_ref, q2_ref, sol_hbm, res_hbm, sol_ref, res_ref, sem):
     step1, ratio, step2 = coef_ref[:, 0:1], coef_ref[:, 1:2], coef_ref[:, 2:3]
-    b, q1 = b_ref[...], q1_ref[...]
-    residual = b - step1 * q1
-    sol_ref[...] = step1 * b + step2 * (residual + ratio * b)
-    res_ref[...] = residual - step2 * ((1.0 + ratio) * q1 - step1 * q2_ref[...])
+    copies = []
+    for i in range(CHIPS):
+        at = pl.ds(i * bs, bs)
+        b, q1 = b_ref[:, at], q1_ref[:, at]
+        residual = b - step1 * q1
+        sol_ref[:, at] = step1 * b + step2 * (residual + ratio * b)
+        res_ref[:, at] = residual - step2 * ((1.0 + ratio) * q1 - step1 * q2_ref[:, at])
+        copies.append(pltpu.make_async_copy(sol_ref.at[:, at], sol_hbm.at[:, at], sem.at[2 * i]))
+        copies.append(pltpu.make_async_copy(res_ref.at[:, at], res_hbm.at[:, at], sem.at[2 * i + 1]))
+        copies[-2].start()
+        copies[-1].start()
+    for copy in copies:
+        copy.wait()
 
 
 def body(features, inv_scale, signal, noise_var, right_side, block_pairs):
@@ -598,14 +602,15 @@
     dma = pltpu.SemaphoreType.DMA
     f32, bf16 = jnp.float32, jnp.bfloat16
     hbm = pl.BlockSpec(memory_space=pl.ANY)
+    on_chip = pl.BlockSpec(memory_space=pltpu.VMEM)
     smem = pl.BlockSpec(memory_space=pltpu.SMEM)
     shape = jax.ShapeDtypeStruct(right_side.shape, f32)
     q1, q2, coef = pl.pallas_call(
         functools.partial(kernel, nx, nz, bs),
         name="conjugate_gradients",
-        out_shape=(shape, shape, jax.ShapeDtypeStruct((R, 128), f32)),
+        out_shape=(vmem(right_side.shape, f32), vmem(right_side.shape, f32), vmem((R, 128), f32)),
         in_specs=[hbm, pl.BlockSpec(memory_space=pltpu.VMEM), smem, hbm, hbm, smem],
-        out_specs=(hbm, hbm, pl.BlockSpec(memory_space=pltpu.VMEM)),
+        out_specs=(on_chip,) * 3,
         scratch_shapes=[
             vmem((F, 3 * bs), f32),
             vmem((3 * bs, TERMS), bf16),
@@ -629,7 +634,6 @@
             vmem((1, nz, 8, 128), f32),
             vmem((1, own), f32),
             dma((6,)),
-            dma((2,)),
             dma((8,)),
             dma((2, 2, 2)),
             dma((2, own // LANES)),
@@ -645,14 +649,14 @@
             collective_id=0, has_side_effects=True, vmem_limit_bytes=60 * 1024 * 1024
         ),
     )(features, inv_scale.reshape(1, -1), signal, noise_var.reshape(1, -1), right_side, block_pairs)
-    blocks = pl.BlockSpec((R, bs), lambda i: (0, i))
     return pl.pallas_call(
-        combine,
+        functools.partial(combine, bs),
         name="combine",
-        grid=(CHIPS,),
         out_shape=(shape, shape),
-        in_specs=[pl.BlockSpec((R, 128), lambda i: (0, 0)), blocks, blocks, blocks],
-        out_specs=(blocks, blocks),
+        in_specs=[on_chip] * 4,
+        out_specs=(hbm, hbm),
+        scratch_shapes=[vmem(right_side.shape, f32), vmem(right_side.shape, f32), dma((2 * CHIPS,))],
+        compiler_params=pltpu.CompilerParams(vmem_limit_bytes=16 * 1024 * 1024),
     )(coef, right_side, q1, q2)
 
 

time: 60.3 us -> 57 us (0.945)
  Pallas kernels: 58.8 us -> 55.5 us
    pallas_call x1, Pallas kernels: 4.33 us -> 1.58 us  [body(): pl.pallas_call(functools.partial(combine, bs), name='combine', out_shape=...]
    pallas_call x1, Pallas kernels: 54.5 us -> 53.9 us  [body(): pl.pallas_call(functools.partial(kernel, nx, nz, bs), name='conjugate_gra...]
where the time goes in v5:
time: 57 us; the launch traced here: 56.9 us
  Pallas kernels  55.5 us (97%)
  between operations  1.39 us (2%)
    pallas_call x1, Pallas kernels, body(): pl.pallas_call(functools.partial(kernel, nx, nz, bs), name='conjugate_gra...  53.9 us
    pallas_call x1, Pallas kernels, body(): pl.pallas_call(functools.partial(combine, bs), name='combine', out_shape=...  1.58 us

profile of v5, /device:TPU:1, one launch (start us, length us, event | category | flops | bytes accessed | tf_op | source)
XLA Modules:
  0.0 56.9 jit_solution(9048691449043584433)
XLA Ops:
  0.6 0.0 copy-start
  1.4 53.9 %conjugate_gradients.1 = (f32[32,8192]{1,0:T(8,128)S(1)}, f32[32,8192]{1,0:T(8,128)S(1)}, f32[32,128]{1,0:T(8,128)S(1)}) custom-call(f32[64,8192]{1,0:T(8,128)} %x_hbm.1, f32[1,64]{1,0:T(1,128)} %bitcast.3, f32[1]{0:T(128)S(6)} %copy.8.sig_ref, f32[1,8192]{1,0:T(1,128)} %bitcast.2, f32[32,8192]{1,0:T(8,128)} %b_ref.1, s32[2,2]{1,0:T(2,128)} %pairs_ref.1), custom_call_target="tpu_custom_call" | custom-call | tf_op jit(solution)/shard_map/conjugate_gradients/pallas_call | solution.py:608
  55.3 0.0 copy-done
  55.3 1.6 %combine.1 = (f32[32,8192]{1,0:T(8,128)}, f32[32,8192]{1,0:T(8,128)}) custom-call(f32[32,128]{1,0:T(8,128)S(1)} %get-tuple-element.5.coef_ref, f32[32,8192]{1,0:T(8,128)S(1)} %copy-done, f32[32,8192]{1,0:T(8,128)S(1)} %get-tuple-element.6.q1_ref, f32[32,8192]{1,0:T(8,128)S(1)} %get-tuple-element.7.q2_ref), custom_call_target="tpu_custom_call" | custom-call | tf_op jit(solution)/shard_map/combine/pallas_call | solution.py:652
Async XLA Ops:
  0.6 54.6 %copy-start = (f32[32,8192]{1,0:T(8,128)S(1)}, f32[32,8192]{1,0:T(8,128)}, u32[]{:S(2)}) copy-start(f32[32,8192]{1,0:T(8,128)} %b_ref.1) | copy-start | bytes 3145732
